TPU v7x, 32 devices: a whole 2x2x4 slice. The times are simulated.
32 devices in a mesh: strip: 8 (over z, x), col: 4 (over y, core).
Axes of the slice: x: 2, y: 2, z: 4, core: 2. Of those that a mesh axis runs over, the one named last changes fastest.
Arguments:
- residuals: float32 [16, 64, 2560], P('strip'), may hold values from -6 to 6
- corr_rows: float32 [64], replicated, may hold values from 0.5 to 2
- corr_cols: float32 [2560], replicated, may hold values from 0.5 to 2
- row_anchor: int32 [16], replicated, may hold values from 0 to 64
- col_anchor: int32 [16], replicated, may hold values from 0 to 7680
- valid_first: int32 [16], replicated, may hold values from 0 to 15
- valid_end: int32 [16], replicated, may hold values from 49 to 64
- facet_of_slot: int32 [16], replicated, may hold values from 0 to 15, each once
Outputs:
- stitched: float32 [128, 10240], P('strip', 'col')
- column_power: float32 [10240], P('col')
Inputs may be any that keep to these rules, and one draw needn't show every extreme that they name: facet_of_slot names each of the 16 facets exactly once.
All inputs are finite; a program needn't handle non-finite values.
Results may differ from a plain program's by a relative error of at most 0.0003.
Values sent between devices are 32-bit elements; how exact they have to be, the bound alone decides.
A program may use at most 64 MiB of HBM per device.

v0:
```python
import functools
import math

import jax
import jax.numpy as jnp
from jax import lax
from jax.experimental import pallas as pl
from jax.experimental.pallas import tpu as pltpu
from jax.sharding import PartitionSpec as P

MESH = pl.DeviceIdType.MESH
CHUNKS = 4


def taper(position, count):
    angle = (position.astype(jnp.float32) + (0.5 - count / 2)) * (math.pi / count)
    square = angle * angle
    value = jnp.full_like(square, 1.0 / math.factorial(12))
    for order in (10, 8, 6, 4, 2, 0):
        sign = -1.0 if order % 4 == 2 else 1.0
        value = value * square + sign / math.factorial(order)
    return value * value


def visit_order(count):
    return [sorted(range(count), key=lambda d: (-abs(d - z), d < z)) for z in range(count)]


def place_kernel(
    strips, lanes, table_ref, rows_ref, cols_ref, res_ref,
    blocks_ref, placed,
):
    local, fh, fw = res_ref.shape
    height = fh // 4
    width = fw // CHUNKS
    strip = lax.axis_index("strip")
    group = lax.axis_index("col")

    eye = lax.broadcasted_iota(jnp.int32, (fh, fh), 0) == lax.broadcasted_iota(
        jnp.int32, (fh, fh), 1
    )
    corr_row = jnp.sum(jnp.where(eye, rows_ref[...], 0.0), axis=1, keepdims=True)
    y = lax.broadcasted_iota(jnp.int32, (fh, 1), 0)
    u = lax.broadcasted_iota(jnp.int32, (1, fw), 1)
    row_taper = taper(y, fh)
    corr_col = jnp.concatenate([cols_ref[pl.ds(i, 1), :] for i in range(fw // 128)], axis=1)
    col_scale = taper(u, fw) * corr_col
    blank = jnp.zeros((height, fw), jnp.float32)
    sub = lax.broadcasted_iota(jnp.int32, (8, 1), 0)
    anchors = []
    for p in range(local):
        f = table_ref[0, strip * local + p]
        ra, ca = table_ref[1, f], table_ref[2, f]
        anchors.append(ra)
        inside = (y >= table_ref[3, f]) & (y < table_ref[4, f])
        row_scale = jnp.where(inside, row_taper, 0.0) * corr_row
        col_pos = u + (group * fw - ca)
        col_inside = (col_pos >= 0) & (col_pos < fw)
        shift = lax.rem(ca, fw)
        lift = lax.rem(ra, 8)
        placed[p, pl.ds(0, height), :] = blank
        placed[p, pl.ds(height + fh + 8, height), :] = blank
        held = jnp.zeros((8, fw), jnp.float32)
        for row in range(0, fh, 8):
            term = res_ref[p, pl.ds(row, 8), :] * col_scale * row_scale[row : row + 8]
            term = jnp.where(col_inside, pltpu.roll(term, shift, axis=1), 0.0)
            term = pltpu.roll(term, lift, axis=0)
            placed[p, pl.ds(height + row, 8), :] = jnp.where(sub < lift, held, term)
            held = term
        placed[p, pl.ds(height + fh, 8), :] = jnp.where(sub < lift, held, 0.0)

    def place(block, chunk):
        total = None
        for p in range(local):
            tile = block * (height // 8) - lax.div(anchors[p], 8)
            start = (jnp.clip(tile, -height // 8, fh // 8 + 1) + height // 8) * 8
            start = pl.multiple_of(start, 8)
            part = placed[p, pl.ds(start, height), pl.ds(chunk * width, width)]
            total = part if total is None else total + part
        return total

    for block in range(strips):
        for c in range(CHUNKS):
            blocks_ref[block // lanes, block % lanes, c] = place(block, c)


def kernel(
    strips, lanes, table_ref, blocks_ref,
    out_ref, power_ref, den, xrecv, zsend, zrecv, psend, precv,
    xs_sem, xr_sem, zs_sem, zr_sem, ps_sem, pr_sem,
):
    facets = table_ref.shape[1]
    height, fw = out_ref.shape
    fh = 4 * height
    levels = strips // lanes
    width = fw // CHUNKS
    strip = lax.axis_index("strip")
    group = lax.axis_index("col")
    z, x = lax.div(strip, lanes), lax.rem(strip, lanes)

    barrier = pltpu.get_barrier_semaphore()
    for k in range(1, strips):
        peer = lax.rem(strip + k, strips)
        pl.semaphore_signal(barrier, inc=1, device_id={"strip": peer}, device_id_type=MESH)

    order = visit_order(levels)

    def dest(t):
        d = jnp.int32(order[0][t])
        for place_z in range(1, levels):
            d = jnp.where(z == place_z, jnp.int32(order[place_z][t]), d)
        return d

    def x_copy(k, d, c):
        return pltpu.make_async_remote_copy(
            src_ref=blocks_ref.at[d, lax.rem(x + k, lanes), c],
            dst_ref=xrecv.at[k - 1, d, c],
            send_sem=xs_sem.at[k - 1, d, c],
            recv_sem=xr_sem.at[k - 1, d, c],
            device_id={"strip": z * lanes + lax.rem(x + k, lanes)},
            device_id_type=MESH,
        )

    def z_copy(way, d, c, target):
        return pltpu.make_async_remote_copy(
            src_ref=zsend.at[d, c],
            dst_ref=zrecv.at[way, d, c],
            send_sem=zs_sem.at[d, c],
            recv_sem=zr_sem.at[way, d, c],
            device_id={"strip": target * lanes + x},
            device_id_type=MESH,
        )

    def p_copy(k):
        return pltpu.make_async_remote_copy(
            src_ref=psend,
            dst_ref=precv.at[k - 1],
            send_sem=ps_sem.at[k - 1],
            recv_sem=pr_sem.at[k - 1],
            device_id={"strip": lax.rem(strip + k, strips)},
            device_id_type=MESH,
        )

    pl.semaphore_wait(barrier, strips - 1)
    for t in range(levels):
        d = dest(t)
        for c in range(CHUNKS):
            for k in range(1, lanes):
                x_copy(k, d, c).start()

    v = lax.broadcasted_iota(jnp.int32, (height, 1), 0) + strip * height
    u8 = lax.broadcasted_iota(jnp.int32, (8, fw), 1) + group * fw

    den[...] = jnp.zeros_like(den)

    def add_facet(f, carry):
        row_pos = v - table_ref[1, f]
        row_inside = (row_pos >= table_ref[3, f]) & (row_pos < table_ref[4, f])
        row_part = jnp.where(row_inside, taper(row_pos, fh), 0.0)
        col_pos = u8 - table_ref[2, f]
        col_inside = (col_pos >= 0) & (col_pos < fw)
        col_part = jnp.where(col_inside, taper(col_pos, fw), 0.0)
        for row in range(0, height, 8):
            den[pl.ds(row, 8), :] += row_part[row : row + 8] * col_part
        return carry

    lax.fori_loop(0, facets, add_facet, 0)

    def gather_x(d, c):
        total = blocks_ref[d, x, c]
        for k in range(1, lanes):
            x_copy(k, d, c).wait_recv()
            total = total + xrecv[k - 1, d, c]
        return total

    for t in range(levels - 1):
        d = dest(t)
        right = d > z
        way = jnp.where(right, 0, 1)
        target = jnp.where(right, z + 1, z - 1)
        fed = jnp.where(right, z > 0, z < levels - 1)
        for c in range(CHUNKS):
            zsend[d, c] = gather_x(d, c)

            @pl.when(fed)
            def _():
                z_copy(way, d, c, target).wait_recv()
                zsend[d, c] += zrecv[way, d, c]

            z_copy(way, d, c, target).start()

    for c in range(CHUNKS):
        columns = pl.ds(c * width, width)
        out_ref[:, columns] = gather_x(z, c)

        @pl.when(z > 0)
        def _():
            z_copy(0, z, c, z - 1).wait_recv()
            out_ref[:, columns] += zrecv[0, z, c]

        @pl.when(z < levels - 1)
        def _():
            z_copy(1, z, c, z + 1).wait_recv()
            out_ref[:, columns] += zrecv[1, z, c]

        stitched = out_ref[:, columns] / jnp.maximum(den[:, columns], 0.5)
        out_ref[:, columns] = stitched
        psend[:, columns] = jnp.sum(stitched * stitched, axis=0, keepdims=True)

    for k in range(1, strips):
        p_copy(k).start()
    total = psend[...]
    for k in range(1, strips):
        p_copy(k).wait_recv()
        total = total + precv[k - 1]
    total = total * (1.0 / (strips * height))
    for row in range(fw // 128):
        power_ref[pl.ds(row, 1), :] = total[:, row * 128 : (row + 1) * 128]

    for k in range(1, strips):
        p_copy(k).wait_send()
    for t in range(levels):
        d = dest(t)
        for c in range(CHUNKS):
            for k in range(1, lanes):
                x_copy(k, d, c).wait_send()
            if t < levels - 1:
                z_copy(0, d, c, jnp.where(d > z, z + 1, z - 1)).wait_send()


def body(strips, lanes, residuals, corr_rows, corr_cols, row_anchor, col_anchor, first, end, slots):
    local, fh, fw = residuals.shape
    height = fh // 4
    levels = strips // lanes
    width = fw // CHUNKS
    others = max(lanes - 1, 1)
    smem = pl.BlockSpec(memory_space=pltpu.SMEM)
    vmem = pl.BlockSpec(memory_space=pltpu.VMEM)
    dma = pltpu.SemaphoreType.DMA
    table = jnp.stack([slots, row_anchor, col_anchor, first, end])
    block_bytes = 4 * height * fw
    margin = 4 * 1024 * 1024
    blocks = pl.pallas_call(
        functools.partial(place_kernel, strips, lanes),
        out_shape=jax.ShapeDtypeStruct((levels, lanes, CHUNKS, height, width), jnp.float32),
        in_specs=[smem] + [vmem] * 3,
        out_specs=vmem,
        scratch_shapes=[pltpu.VMEM((local, fh + 8 + 2 * height, fw), jnp.float32)],
        compiler_params=pltpu.CompilerParams(
            vmem_limit_bytes=(strips + 11 * local) * block_bytes + margin
        ),
    )(table, corr_rows[None, :], corr_cols.reshape(fw // 128, 128), residuals)
    stitched, power = pl.pallas_call(
        functools.partial(kernel, strips, lanes),
        out_shape=(
            jax.ShapeDtypeStruct((height, fw), jnp.float32),
            jax.ShapeDtypeStruct((fw // 128, 128), jnp.float32),
        ),
        in_specs=[smem, vmem],
        out_specs=(vmem, vmem),
        scratch_shapes=[
            pltpu.VMEM((height, fw), jnp.float32),
            pltpu.VMEM((others, levels, CHUNKS, height, width), jnp.float32),
            pltpu.VMEM((levels, CHUNKS, height, width), jnp.float32),
            pltpu.VMEM((2, levels, CHUNKS, height, width), jnp.float32),
            pltpu.VMEM((1, fw), jnp.float32),
            pltpu.VMEM((strips - 1, 1, fw), jnp.float32),
            dma((others, levels, CHUNKS)),
            dma((others, levels, CHUNKS)),
            dma((levels, CHUNKS)),
            dma((2, levels, CHUNKS)),
            dma((strips - 1,)),
            dma((strips - 1,)),
        ],
        compiler_params=pltpu.CompilerParams(
            collective_id=0,
            has_side_effects=True,
            vmem_limit_bytes=(2 * strips + 3 * levels + 4) * block_bytes + margin,
        ),
    )(table, blocks)
    return stitched, power.reshape(fw)


def solution(mesh):
    strips = mesh.shape["strip"]
    lanes = math.gcd(strips, max(mesh.shape["col"] // 2, 1))
    in_specs = (P("strip", None, None), P(), P(), P(), P(), P(), P(), P())
    out_specs = (P("strip", "col"), P("col"))
    run = functools.partial(body, strips, lanes)
    return jax.shard_map(run, mesh=mesh, in_specs=in_specs, out_specs=out_specs, check_vma=False)
```

profile of v0, /device:TPU:0, one launch (start us, length us, event | category | flops | bytes accessed | tf_op | source)
XLA Modules:
  0.0 35.6 jit_solution(14901899768821543534)
XLA Ops:
  0.6 0.7 %stack.23.table_ref = s32[5,16]{1,0:T(8,128)S(1)} concatenate(s32[1,16]{1,0:T(1,128)} %bitcast.11, s32[1,16]{1,0:T(1,128)} %bitcast.12, s32[1,16]{1,0:T(1,128)} %bitcast.13, s32[1,16]{1,0:T(1,128)} %bitcast.14, s32[1,16]{1,0:T(1,128)} %bitcast.15), dimensions={0} | concatenate | bytes 640 | tf_op jit(solution)/shard_map/stack | solution.py:240
  1.4 0.0 copy-start
  1.4 1.3 %copy-done = f32[2,64,2560]{2,1,0:T(8,128)S(1)} copy-done((f32[2,64,2560]{2,1,0:T(8,128)S(1)}, f32[2,64,2560]{2,1,0:T(8,128)}, u32[]{:S(2)}) %copy-start) | copy-done | bytes 1310744
  2.7 0.0 copy-start.1
  2.7 0.7 %copy-done.1 = f32[2560]{0:T(1024)S(1)} copy-done((f32[2560]{0:T(1024)S(1)}, f32[2560]{0:T(1024)}, u32[]{:S(2)}) %copy-start.1) | copy-done | bytes 10264
  3.4 0.0 copy-start.2
  3.4 0.7 %copy-done.2 = f32[64]{0:T(128)S(1)} copy-done((f32[64]{0:T(128)S(1)}, f32[64]{0:T(128)}, u32[]{:S(2)}) %copy-start.2) | copy-done | bytes 280
  4.0 1.7 %shard_map.95.blocks_ref = f32[4,2,4,16,640]{4,3,2,1,0:T(8,128)S(1)} custom-call(s32[5,16]{1,0:T(8,128)S(1)} %stack.23.table_ref, f32[1,64]{1,0:T(1,128)S(1)} %bitcast.10, f32[20,128]{1,0:T(8,128)S(1)} %bitcast.8, f32[2,64,2560]{2,1,0:T(8,128)S(1)} %copy-done), custom_call_target="tpu_custom_call" | custom-call | tf_op jit(solution)/shard_map/pallas_call | solution.py:243
  5.8 28.5 %shard_map.96 = (f32[16,2560]{1,0:T(8,128)S(1)}, f32[20,128]{1,0:T(8,128)S(1)}) custom-call(s32[5,16]{1,0:T(8,128)S(1)} %stack.23.table_ref, f32[4,2,4,16,640]{4,3,2,1,0:T(8,128)S(1)} %shard_map.95.blocks_ref), custom_call_target="tpu_custom_call" | custom-call | tf_op jit(solution)/shard_map/pallas_call | solution.py:253
  34.3 0.7 %copy.12 = f32[16,2560]{1,0:T(8,128)} copy(f32[16,2560]{1,0:T(8,128)S(1)} %get-tuple-element.8) | data formatting | bytes 327680
  35.0 0.6 %copy.13 = f32[2560]{0:T(1024)} copy(f32[2560]{0:T(1024)S(1)} %bitcast.9) | data formatting | bytes 20480
Async XLA Ops:
  1.4 1.3 %copy-start = (f32[2,64,2560]{2,1,0:T(8,128)S(1)}, f32[2,64,2560]{2,1,0:T(8,128)}, u32[]{:S(2)}) copy-start(f32[2,64,2560]{2,1,0:T(8,128)} %res_ref.1) | copy-start | bytes 3932164
  2.7 0.7 %copy-start.1 = (f32[2560]{0:T(1024)S(1)}, f32[2560]{0:T(1024)}, u32[]{:S(2)}) copy-start(f32[2560]{0:T(1024)} %param.10) | copy-start | bytes 30724
  3.4 0.7 %copy-start.2 = (f32[64]{0:T(128)S(1)}, f32[64]{0:T(128)}, u32[]{:S(2)}) copy-start(f32[64]{0:T(128)} %param.9) | copy-start | bytes 772
where the time goes:
time: 35.8 us; the launch traced here: 35.6 us
  Pallas kernels  30.3 us (85%)
  local copies, waits for them, and re-layouts  4.68 us (13%)
  between operations  0.65 us (2%)
    pallas_call x1, Pallas kernels, body(): pl.pallas_call(functools.partial(kernel, strips, lanes), out_shape=(jax.S...  28.5 us
    unnamed x8, local copies, waits for them, and re-layouts  3.95 us
    pallas_call x1, Pallas kernels, body(): pl.pallas_call(functools.partial(place_kernel, strips, lanes), out_shape=...  1.71 us
    another operation x1, local copies, waits for them, and re-layouts, body(): table = jnp.stack([slots, row_anchor, col_anchor, first, end])  0.74 us

commit v1 on v0

v1 whole, which is shorter than its diff:
```python
import functools
import math

import jax
import jax.numpy as jnp
from jax import lax
from jax.experimental import pallas as pl
from jax.experimental.pallas import tpu as pltpu
from jax.sharding import PartitionSpec as P

MESH = pl.DeviceIdType.MESH
CHUNKS = 4
EARLY = 0.15
TILE = 128


def taper(position, count):
    angle = (position.astype(jnp.float32) + (0.5 - count / 2)) * (math.pi / count)
    square = angle * angle
    value = jnp.full_like(square, 1.0 / math.factorial(12))
    for order in (10, 8, 6, 4, 2, 0):
        sign = -1.0 if order % 4 == 2 else 1.0
        value = value * square + sign / math.factorial(order)
    return value * value


def visit_order(count):
    return [sorted(range(count), key=lambda d: (-abs(d - z), d < z)) for z in range(count)]


def column_chunks(tiles, first):
    edges = [first + (tiles - first) * c // CHUNKS for c in range(CHUNKS + 1)]
    return [(a, b - a) for a, b in zip(edges, edges[1:]) if b > a]


def kernel(
    strips, lanes,
    slots_ref, row_ref, col_ref, first_ref, end_ref, rows_hbm, cols_hbm, res_hbm,
    out_ref, power_ref,
    res_ref, rows_ref, cols_ref, rolled, blocks, inv, xrecv, zsend, zrecv,
    fsend, frecv, fkeep, fxsend, fxrecv, psend, precv,
    in_sem, xs_sem, xr_sem, zs_sem, zr_sem, fs_sem, fr_sem, gs_sem, gr_sem, ps_sem, pr_sem,
):
    local, fh, fw = res_ref.shape
    facets = slots_ref.shape[0]
    height = out_ref.shape[0]
    levels = strips // lanes
    tiles = fw // TILE
    early = fsend.shape[2]
    chunks = column_chunks(tiles, early)
    parts = [(0, early)] + chunks
    strip = lax.axis_index("strip")
    group = lax.axis_index("col")
    z, x = lax.div(strip, lanes), lax.rem(strip, lanes)

    loads = [
        pltpu.make_async_copy(rows_hbm, rows_ref, in_sem.at[0]),
        pltpu.make_async_copy(cols_hbm, cols_ref, in_sem.at[1]),
    ] + [
        pltpu.make_async_copy(res_hbm.at[p], res_ref.at[p], in_sem.at[2 + p])
        for p in range(local)
    ]
    for load in loads:
        load.start()

    barrier = pltpu.get_barrier_semaphore()
    for k in range(1, strips):
        peer = lax.rem(strip + k, strips)
        pl.semaphore_signal(barrier, inc=1, device_id={"strip": peer}, device_id_type=MESH)

    order = visit_order(levels)

    def dest(t):
        d = jnp.int32(order[0][t])
        for place_z in range(1, levels):
            d = jnp.where(z == place_z, jnp.int32(order[place_z][t]), d)
        return d

    def lane_of(k):
        return lax.rem(x + k, lanes)

    def span(c):
        return pl.ds(chunks[c][0], chunks[c][1])

    def x_copy(k, d, c):
        return pltpu.make_async_remote_copy(
            src_ref=blocks.at[d, lane_of(k), span(c)],
            dst_ref=xrecv.at[k - 1, d, span(c)],
            send_sem=xs_sem.at[k - 1, d, c],
            recv_sem=xr_sem.at[k - 1, d, c],
            device_id={"strip": z * lanes + lane_of(k)},
            device_id_type=MESH,
        )

    def z_copy(way, d, c, target):
        return pltpu.make_async_remote_copy(
            src_ref=zsend.at[d, span(c)],
            dst_ref=zrecv.at[way, d, span(c)],
            send_sem=zs_sem.at[d, c],
            recv_sem=zr_sem.at[way, d, c],
            device_id={"strip": target * lanes + x},
            device_id_type=MESH,
        )

    def f_copy(way, d, target):
        return pltpu.make_async_remote_copy(
            src_ref=fsend.at[d],
            dst_ref=frecv.at[way, d],
            send_sem=fs_sem.at[d],
            recv_sem=fr_sem.at[way, d],
            device_id={"strip": target * lanes + x},
            device_id_type=MESH,
        )

    def g_copy(k):
        return pltpu.make_async_remote_copy(
            src_ref=fxsend.at[k - 1],
            dst_ref=fxrecv.at[k - 1],
            send_sem=gs_sem.at[k - 1],
            recv_sem=gr_sem.at[k - 1],
            device_id={"strip": z * lanes + lane_of(k)},
            device_id_type=MESH,
        )

    def p_copy(k, i):
        return pltpu.make_async_remote_copy(
            src_ref=psend.at[pl.ds(*parts[i])],
            dst_ref=precv.at[k - 1, pl.ds(*parts[i])],
            send_sem=ps_sem.at[k - 1, i],
            recv_sem=pr_sem.at[k - 1, i],
            device_id={"strip": lax.rem(strip + k, strips)},
            device_id_type=MESH,
        )

    eye = lax.broadcasted_iota(jnp.int32, (fh, fh), 0) == lax.broadcasted_iota(
        jnp.int32, (fh, fh), 1
    )
    y = lax.broadcasted_iota(jnp.int32, (fh, 1), 0)
    u = lax.broadcasted_iota(jnp.int32, (1, fw), 1)
    row_taper = taper(y, fh)
    col_taper = taper(u, fw)
    loads[0].wait()
    loads[1].wait()
    corr_row = jnp.sum(jnp.where(eye, rows_ref[...], 0.0), axis=1, keepdims=True)
    corr_col = jnp.concatenate([cols_ref[pl.ds(i, 1), :] for i in range(tiles)], axis=1)
    col_scale = col_taper * corr_col
    anchors = []
    for p in range(local):
        f = slots_ref[strip * local + p]
        ra, ca = row_ref[f], col_ref[f]
        anchors.append(ra)
        inside = (y >= first_ref[f]) & (y < end_ref[f])
        row_scale = jnp.where(inside, row_taper, 0.0) * corr_row
        col_pos = u + (group * fw - ca)
        col_inside = (col_pos >= 0) & (col_pos < fw)
        shift = lax.rem(ca, fw)
        loads[2 + p].wait()
        for row in range(0, fh, 8):
            term = res_ref[p, pl.ds(row, 8), :] * col_scale * row_scale[row : row + 8]
            rolled[p, pl.ds(row, 8), :] = jnp.where(col_inside, pltpu.roll(term, shift, axis=1), 0.0)
    spare = jnp.zeros((strips * height - fh, TILE), jnp.float32)
    for j in range(tiles):
        total = None
        for p in range(local):
            piece = jnp.concatenate([rolled[p, :, pl.ds(j * TILE, TILE)], spare], axis=0)
            piece = pltpu.roll(piece, anchors[p], axis=0)
            total = piece if total is None else total + piece
        for s in range(strips):
            blocks[s // lanes, s % lanes, j] = total[s * height : (s + 1) * height]

    pl.semaphore_wait(barrier, strips - 1)
    for t in range(levels - 1):
        d = dest(t)
        right = d > z
        fed = jnp.where(right, z > 0, z < levels - 1)
        fsend[d] = blocks[d, :, pl.ds(0, early)]

        @pl.when(jnp.logical_not(fed))
        def _():
            f_copy(jnp.where(right, 0, 1), d, jnp.where(right, z + 1, z - 1)).start()

    for t in range(levels):
        d = dest(t)
        for c in range(len(chunks)):
            for k in range(1, lanes):
                x_copy(k, d, c).start()

    v = lax.broadcasted_iota(jnp.int32, (height, 1), 0) + strip * height
    u8 = lax.broadcasted_iota(jnp.int32, (8, fw), 1) + group * fw
    inv[...] = jnp.zeros_like(inv)

    def add_facet(f, carry):
        row_pos = v - row_ref[f]
        row_inside = (row_pos >= first_ref[f]) & (row_pos < end_ref[f])
        row_part = jnp.where(row_inside, taper(row_pos, fh), 0.0)
        col_pos = u8 - col_ref[f]
        col_inside = (col_pos >= 0) & (col_pos < fw)
        col_part = jnp.where(col_inside, taper(col_pos, fw), 0.0)
        for j in range(tiles):
            for row in range(0, height, 8):
                inv[j, pl.ds(row, 8), :] += (
                    row_part[row : row + 8] * col_part[:, j * TILE : (j + 1) * TILE]
                )
        return carry

    lax.fori_loop(0, facets, add_facet, 0)
    inv[...] = 1.0 / jnp.maximum(inv[...], 0.5)

    def gather_x(d, c):
        total = blocks[d, x, span(c)]
        for k in range(1, lanes):
            x_copy(k, d, c).wait_recv()
            total = total + xrecv[k - 1, d, span(c)]
        return total

    def pass_early(t):
        d = dest(t)
        right = d > z
        way = jnp.where(right, 0, 1)
        target = jnp.where(right, z + 1, z - 1)
        fed = jnp.where(right, z > 0, z < levels - 1)

        @pl.when(fed)
        def _():
            f_copy(way, d, target).wait_recv()
            fsend[d] += frecv[way, d]
            f_copy(way, d, target).start()

    def pass_rest(t):
        d = dest(t)
        right = d > z
        way = jnp.where(right, 0, 1)
        target = jnp.where(right, z + 1, z - 1)
        fed = jnp.where(right, z > 0, z < levels - 1)
        for c in range(len(chunks)):
            zsend[d, span(c)] = gather_x(d, c)

            @pl.when(fed)
            def _():
                z_copy(way, d, c, target).wait_recv()
                zsend[d, span(c)] += zrecv[way, d, span(c)]

            z_copy(way, d, c, target).start()

    def swap_early():
        fkeep[...] = blocks[z, :, pl.ds(0, early)]

        @pl.when(z > 0)
        def _():
            f_copy(0, z, z - 1).wait_recv()
            fkeep[...] += frecv[0, z]

        @pl.when(z < levels - 1)
        def _():
            f_copy(1, z, z + 1).wait_recv()
            fkeep[...] += frecv[1, z]

        for k in range(1, lanes):
            fxsend[k - 1] = fkeep[lane_of(k)]
        for k in range(1, lanes):
            g_copy(k).start()

    def settle(i, total):
        first, count = parts[i]
        stitched = total * inv[pl.ds(first, count)]
        for j in range(count):
            out_ref[:, pl.ds((first + j) * TILE, TILE)] = stitched[j]
        psend[pl.ds(first, count)] = jnp.sum(stitched * stitched, axis=1, keepdims=True)
        for k in range(1, strips):
            p_copy(k, i).start()

    for t in range(levels - 1):
        if t == 0:
            pass_early(0)
        if t == min(1, levels - 2):
            for later in range(1, levels - 1):
                pass_early(later)
        if t == levels - 2:
            swap_early()
        pass_rest(t)

    for c in range(len(chunks)):
        zsend[z, span(c)] = gather_x(z, c)

        @pl.when(z > 0)
        def _():
            z_copy(0, z, c, z - 1).wait_recv()
            zsend[z, span(c)] += zrecv[0, z, span(c)]

        @pl.when(z < levels - 1)
        def _():
            z_copy(1, z, c, z + 1).wait_recv()
            zsend[z, span(c)] += zrecv[1, z, span(c)]

        settle(1 + c, zsend[z, span(c)])
    total = fkeep[x]
    for k in range(1, lanes):
        g_copy(k).wait_recv()
        total = total + fxrecv[k - 1]
    settle(0, total)

    for i in range(len(parts)):
        for k in range(1, strips):
            p_copy(k, i).wait_recv()
    total = psend[...]
    for k in range(1, strips):
        total = total + precv[k - 1]
    total = total * (1.0 / (strips * height))
    for j in range(tiles):
        power_ref[pl.ds(j, 1), :] = total[j]

    for i in range(len(parts)):
        for k in range(1, strips):
            p_copy(k, i).wait_send()
    for k in range(1, lanes):
        g_copy(k).wait_send()
    for t in range(levels):
        d = dest(t)
        target = jnp.where(d > z, z + 1, z - 1)
        for c in range(len(chunks)):
            for k in range(1, lanes):
                x_copy(k, d, c).wait_send()
            if t < levels - 1:
                z_copy(0, d, c, target).wait_send()
        if t < levels - 1:
            f_copy(0, d, target).wait_send()


def finish(stitched_ref, power_ref, out_ref, power_out, sems):
    copies = [
        pltpu.make_async_copy(stitched_ref, out_ref, sems.at[0]),
        pltpu.make_async_copy(power_ref, power_out, sems.at[1]),
    ]
    for copy in copies:
        copy.start()
    for copy in copies:
        copy.wait()


def body(strips, lanes, residuals, corr_rows, corr_cols, row_anchor, col_anchor, first, end, slots):
    local, fh, fw = residuals.shape
    height = fh // 4
    levels = strips // lanes
    others = max(lanes - 1, 1)
    smem = pl.BlockSpec(memory_space=pltpu.SMEM)
    vmem = pl.BlockSpec(memory_space=pltpu.VMEM)
    hbm = pl.BlockSpec(memory_space=pltpu.HBM)
    dma = pltpu.SemaphoreType.DMA
    tiles = fw // TILE
    early = max(round(EARLY * tiles), 1)
    chunks = len(column_chunks(tiles, early))
    block_bytes = 4 * height * fw
    margin = 4 * 1024 * 1024
    blocks = 8 * local + (2 + others) * strips + 4 * levels + 4
    stitched, power = pl.pallas_call(
        functools.partial(kernel, strips, lanes),
        out_shape=(
            jax.ShapeDtypeStruct((height, fw), jnp.float32),
            jax.ShapeDtypeStruct((tiles, TILE), jnp.float32),
        ),
        in_specs=[smem] * 5 + [hbm] * 3,
        out_specs=(vmem, vmem),
        scratch_shapes=[
            pltpu.VMEM((local, fh, fw), jnp.float32),
            pltpu.VMEM((1, fh), jnp.float32),
            pltpu.VMEM((tiles, TILE), jnp.float32),
            pltpu.VMEM((local, fh, fw), jnp.float32),
            pltpu.VMEM((levels, lanes, tiles, height, TILE), jnp.float32),
            pltpu.VMEM((tiles, height, TILE), jnp.float32),
            pltpu.VMEM((others, levels, tiles, height, TILE), jnp.float32),
            pltpu.VMEM((levels, tiles, height, TILE), jnp.float32),
            pltpu.VMEM((2, levels, tiles, height, TILE), jnp.float32),
            pltpu.VMEM((levels, lanes, early, height, TILE), jnp.float32),
            pltpu.VMEM((2, levels, lanes, early, height, TILE), jnp.float32),
            pltpu.VMEM((lanes, early, height, TILE), jnp.float32),
            pltpu.VMEM((others, early, height, TILE), jnp.float32),
            pltpu.VMEM((others, early, height, TILE), jnp.float32),
            pltpu.VMEM((tiles, 1, TILE), jnp.float32),
            pltpu.VMEM((strips - 1, tiles, 1, TILE), jnp.float32),
            dma((2 + local,)),
            dma((others, levels, chunks)),
            dma((others, levels, chunks)),
            dma((levels, chunks)),
            dma((2, levels, chunks)),
            dma((levels,)),
            dma((2, levels)),
            dma((others,)),
            dma((others,)),
            dma((strips - 1, chunks + 1)),
            dma((strips - 1, chunks + 1)),
        ],
        compiler_params=pltpu.CompilerParams(
            collective_id=0,
            has_side_effects=True,
            vmem_limit_bytes=blocks * block_bytes + margin,
        ),
    )(*(
        pltpu.with_memory_space_constraint(operand, pltpu.HBM)
        for operand in (
            slots, row_anchor, col_anchor, first, end,
            corr_rows[None, :], corr_cols.reshape(fw // TILE, TILE), residuals,
        )
    ))
    stitched, power = pl.pallas_call(
        finish,
        out_shape=(
            jax.ShapeDtypeStruct((height, fw), jnp.float32),
            jax.ShapeDtypeStruct((fw // TILE, TILE), jnp.float32),
        ),
        in_specs=[vmem, vmem],
        out_specs=(hbm, hbm),
        scratch_shapes=[dma((2,))],
    )(*(pltpu.with_memory_space_constraint(part, pltpu.VMEM) for part in (stitched, power)))
    return stitched, power.reshape(fw)


def solution(mesh):
    strips = mesh.shape["strip"]
    lanes = math.gcd(strips, max(mesh.shape["col"] // 2, 1))
    in_specs = (P("strip", None, None), P(), P(), P(), P(), P(), P(), P())
    out_specs = (P("strip", "col"), P("col"))
    run = functools.partial(body, strips, lanes)
    return jax.shard_map(run, mesh=mesh, in_specs=in_specs, out_specs=out_specs, check_vma=False)
```

time: 35.8 us -> 30.2 us (0.84)
  local copies, waits for them, and re-layouts: 4.68 us -> 0 us
  Pallas kernels: 30.3 us -> 29.4 us
    unnamed x8 -> x0, local copies, waits for them, and re-layouts: 3.95 us -> none
    pallas_call x1, Pallas kernels: 1.71 us -> 0.69 us  [body(): pl.pallas_call(finish, out_shape=(jax.ShapeDtypeStruct((height, fw), jnp....]
    another operation x1 -> x0, local copies, waits for them, and re-layouts: 0.74 us -> none  [body(): table = jnp.stack([slots, row_anchor, col_anchor, first, end])]
where the time goes in v1:
time: 30.2 us; the launch traced here: 30 us
  Pallas kernels  29.4 us (97%)
  between operations  0.64 us (2%)
    pallas_call x1, Pallas kernels, body(): pl.pallas_call(functools.partial(kernel, strips, lanes), out_shape=(jax.S...  28.7 us
    pallas_call x1, Pallas kernels, body(): pl.pallas_call(finish, out_shape=(jax.ShapeDtypeStruct((height, fw), jnp....  0.69 us

profile of v1, /device:TPU:0, one launch (start us, length us, event | category | flops | bytes accessed | tf_op | source)
XLA Modules:
  0.0 30.0 jit_solution(17258941371058428266)
XLA Ops:
  0.6 28.7 %shard_map.95 = (f32[16,2560]{1,0:T(8,128)S(1)}, f32[20,128]{1,0:T(8,128)S(1)}) custom-call(s32[16]{0:T(128)} %slots_ref.1, s32[16]{0:T(128)} %row_ref.1, s32[16]{0:T(128)} %col_ref.1, s32[16]{0:T(128)} %first_ref.1, s32[16]{0:T(128)} %end_ref.1, f32[1,64]{1,0:T(1,128)} %bitcast.4, f32[20,128]{1,0:T(8,128)} %bitcast.3, f32[2,64,2560]{2,1,0:T(8,128)} %res_hbm.1), custom_call_target="tpu_custom_call" | custom-call | tf_op jit(solution)/shard_map/pallas_call | solution.py:355
  29.4 0.7 %shard_map.96 = (f32[16,2560]{1,0:T(8,128)}, f32[20,128]{1,0:T(8,128)}) custom-call(f32[16,2560]{1,0:T(8,128)S(1)} %get-tuple-element.6.stitched_ref, f32[20,128]{1,0:T(8,128)S(1)} %get-tuple-element.7.power_ref), custom_call_target="tpu_custom_call" | custom-call | tf_op jit(solution)/shard_map/pallas_call | solution.py:404

commit v2 on v1

--- a/solution.py
+++ b/solution.py
@@ -24,8 +24,15 @@
     return value * value
 
 
-def visit_order(count):
-    return [sorted(range(count), key=lambda d: (-abs(d - z), d < z)) for z in range(count)]
+def fed(levels, z, d):
+    return (z == 1 < d) or (z == levels - 2 > d)
+
+
+def visit_order(levels):
+    return [
+        sorted((d for d in range(levels) if d != z), key=lambda d: (fed(levels, z, d), -abs(d - z)))
+        for z in range(levels)
+    ]
 
 
 def column_chunks(tiles, first):
@@ -35,11 +42,11 @@
 
 def kernel(
     strips, lanes,
-    slots_ref, row_ref, col_ref, first_ref, end_ref, rows_hbm, cols_hbm, res_hbm,
+    slots_hbm, row_hbm, col_hbm, first_hbm, end_hbm, rows_hbm, cols_hbm, res_hbm,
     out_ref, power_ref,
-    res_ref, rows_ref, cols_ref, rolled, blocks, inv, xrecv, zsend, zrecv,
+    slots_ref, row_ref, col_ref, first_ref, end_ref, res_ref, rows_ref, cols_ref, rolled, blocks, inv, xrecv, zsend, zrecv,
     fsend, frecv, fkeep, fxsend, fxrecv, psend, precv,
-    in_sem, xs_sem, xr_sem, zs_sem, zr_sem, fs_sem, fr_sem, gs_sem, gr_sem, ps_sem, pr_sem,
+    line, in_sem, xs_sem, xr_sem, zs_sem, zr_sem, fs_sem, fr_sem, gs_sem, gr_sem, ps_sem, pr_sem,
 ):
     local, fh, fw = res_ref.shape
     facets = slots_ref.shape[0]
@@ -53,28 +60,81 @@
     group = lax.axis_index("col")
     z, x = lax.div(strip, lanes), lax.rem(strip, lanes)
 
+    sources = [
+        (slots_hbm, slots_ref), (row_hbm, row_ref), (col_hbm, col_ref), (first_hbm, first_ref),
+        (end_hbm, end_ref), (rows_hbm, rows_ref), (cols_hbm, cols_ref),
+    ]
+    small = len(sources)
+    sources += [(res_hbm.at[p], res_ref.at[p]) for p in range(local)]
     loads = [
-        pltpu.make_async_copy(rows_hbm, rows_ref, in_sem.at[0]),
-        pltpu.make_async_copy(cols_hbm, cols_ref, in_sem.at[1]),
-    ] + [
-        pltpu.make_async_copy(res_hbm.at[p], res_ref.at[p], in_sem.at[2 + p])
-        for p in range(local)
+        pltpu.make_async_copy(source, target, in_sem.at[i])
+        for i, (source, target) in enumerate(sources)
     ]
     for load in loads:
         load.start()
 
+    low, high = z > 0, z < levels - 1
+    leaf = jnp.logical_not(low & high)
+
+    def at(level, lane):
+        return {"strip": level * lanes + lane}
+
     barrier = pltpu.get_barrier_semaphore()
-    for k in range(1, strips):
-        peer = lax.rem(strip + k, strips)
-        pl.semaphore_signal(barrier, inc=1, device_id={"strip": peer}, device_id_type=MESH)
+    for k in range(1, lanes):
+        pl.semaphore_signal(barrier, device_id=at(z, lax.rem(x + k, lanes)), device_id_type=MESH)
+    for there, step in ((low, -1), (high, 1)):
+
+        @pl.when(there)
+        def _():
+            pl.semaphore_signal(barrier, device_id=at(z + step, x), device_id_type=MESH)
+
+    def enter():
+        pl.semaphore_wait(barrier, lanes - 1 + low.astype(jnp.int32) + high.astype(jnp.int32))
+        for side, there, step in ((0, jnp.logical_not(low) & high, 1), (1, jnp.logical_not(high) & low, -1)):
+
+            @pl.when(there)
+            def _():
+                pl.semaphore_signal(line.at[side], device_id=at(z + step, x), device_id_type=MESH)
+
+    def hear(side, when):
+        @pl.when(when)
+        def _():
+            pl.semaphore_wait(line.at[side], 1)
+
+            @pl.when(high if side == 0 else low)
+            def _():
+                pl.semaphore_signal(
+                    line.at[side], device_id=at(z + (1 if side == 0 else -1), x), device_id_type=MESH
+                )
 
     order = visit_order(levels)
 
+    def pick(values):
+        value = jnp.int32(values[0])
+        for level in range(1, levels):
+            value = jnp.where(z == level, jnp.int32(values[level]), value)
+        return value
+
     def dest(t):
-        d = jnp.int32(order[0][t])
-        for place_z in range(1, levels):
-            d = jnp.where(z == place_z, jnp.int32(order[place_z][t]), d)
-        return d
+        return pick([row[t] for row in order])
+
+    def is_fed(t):
+        return pick([int(fed(levels, level, row[t])) for level, row in enumerate(order)]) == 1
+
+    def route(d):
+        target = jnp.where(z == 0, min(1, levels - 1), jnp.where(high, d, levels - 2))
+        slot = jnp.where(target == d, z, jnp.where(z == 0, levels + d, 2 * levels + d))
+        return target, slot
+
+    def inlet(d):
+        return jnp.where(d > z, levels + d, 2 * levels + d)
+
+    def sources():
+        for level in range(levels):
+            if 0 < level < levels - 1:
+                yield level, z != level
+            elif levels > 1:
+                yield level, z == (1 if level == 0 else levels - 2)
 
     def lane_of(k):
         return lax.rem(x + k, lanes)
@@ -88,27 +148,27 @@
             dst_ref=xrecv.at[k - 1, d, span(c)],
             send_sem=xs_sem.at[k - 1, d, c],
             recv_sem=xr_sem.at[k - 1, d, c],
-            device_id={"strip": z * lanes + lane_of(k)},
+            device_id=at(z, lane_of(k)),
             device_id_type=MESH,
         )
 
-    def z_copy(way, d, c, target):
+    def z_copy(d, c, target, slot):
         return pltpu.make_async_remote_copy(
             src_ref=zsend.at[d, span(c)],
-            dst_ref=zrecv.at[way, d, span(c)],
+            dst_ref=zrecv.at[slot, span(c)],
             send_sem=zs_sem.at[d, c],
-            recv_sem=zr_sem.at[way, d, c],
-            device_id={"strip": target * lanes + x},
+            recv_sem=zr_sem.at[slot, c],
+            device_id=at(target, x),
             device_id_type=MESH,
         )
 
-    def f_copy(way, d, target):
+    def f_copy(d, target, slot, source=None):
         return pltpu.make_async_remote_copy(
-            src_ref=fsend.at[d],
-            dst_ref=frecv.at[way, d],
+            src_ref=fsend.at[d] if source is None else source,
+            dst_ref=frecv.at[slot],
             send_sem=fs_sem.at[d],
-            recv_sem=fr_sem.at[way, d],
-            device_id={"strip": target * lanes + x},
+            recv_sem=fr_sem.at[slot],
+            device_id=at(target, x),
             device_id_type=MESH,
         )
 
@@ -118,7 +178,7 @@
             dst_ref=fxrecv.at[k - 1],
             send_sem=gs_sem.at[k - 1],
             recv_sem=gr_sem.at[k - 1],
-            device_id={"strip": z * lanes + lane_of(k)},
+            device_id=at(z, lane_of(k)),
             device_id_type=MESH,
         )
 
@@ -139,8 +199,8 @@
     u = lax.broadcasted_iota(jnp.int32, (1, fw), 1)
     row_taper = taper(y, fh)
     col_taper = taper(u, fw)
-    loads[0].wait()
-    loads[1].wait()
+    for load in loads[:small]:
+        load.wait()
     corr_row = jnp.sum(jnp.where(eye, rows_ref[...], 0.0), axis=1, keepdims=True)
     corr_col = jnp.concatenate([cols_ref[pl.ds(i, 1), :] for i in range(tiles)], axis=1)
     col_scale = col_taper * corr_col
@@ -154,12 +214,13 @@
         col_pos = u + (group * fw - ca)
         col_inside = (col_pos >= 0) & (col_pos < fw)
         shift = lax.rem(ca, fw)
-        loads[2 + p].wait()
+        loads[small + p].wait()
         for row in range(0, fh, 8):
             term = res_ref[p, pl.ds(row, 8), :] * col_scale * row_scale[row : row + 8]
             rolled[p, pl.ds(row, 8), :] = jnp.where(col_inside, pltpu.roll(term, shift, axis=1), 0.0)
     spare = jnp.zeros((strips * height - fh, TILE), jnp.float32)
-    for j in range(tiles):
+
+    def place(j):
         total = None
         for p in range(local):
             piece = jnp.concatenate([rolled[p, :, pl.ds(j * TILE, TILE)], spare], axis=0)
@@ -168,22 +229,32 @@
         for s in range(strips):
             blocks[s // lanes, s % lanes, j] = total[s * height : (s + 1) * height]
 
-    pl.semaphore_wait(barrier, strips - 1)
-    for t in range(levels - 1):
-        d = dest(t)
-        right = d > z
-        fed = jnp.where(right, z > 0, z < levels - 1)
-        fsend[d] = blocks[d, :, pl.ds(0, early)]
-
-        @pl.when(jnp.logical_not(fed))
-        def _():
-            f_copy(jnp.where(right, 0, 1), d, jnp.where(right, z + 1, z - 1)).start()
-
-    for t in range(levels):
-        d = dest(t)
+    def open_early():
+        for t in range(levels - 1):
+            d = dest(t)
+            target, slot = route(d)
+
+            @pl.when(jnp.logical_not(is_fed(t)))
+            def _():
+                f_copy(d, target, slot, blocks.at[d, :, pl.ds(0, early)]).start()
+
+    for i, (first, count) in enumerate(parts):
+        for j in range(first, first + count):
+            place(j)
+            if j == first and i == 1:
+                enter()
+                open_early()
+            if j == first and i > 1:
+                for k in range(1, lanes):
+                    x_copy(k, dest(0), i - 2).start()
+    for k in range(1, lanes):
+        x_copy(k, dest(0), len(chunks) - 1).start()
+    for t in range(1, levels):
         for c in range(len(chunks)):
             for k in range(1, lanes):
-                x_copy(k, d, c).start()
+                x_copy(k, dest(t) if t < levels - 1 else z, c).start()
+    hear(0, (z == 1) & high)
+    hear(1, (z == levels - 2) & low)
 
     v = lax.broadcasted_iota(jnp.int32, (height, 1), 0) + strip * height
     u8 = lax.broadcasted_iota(jnp.int32, (8, fw), 1) + group * fw
@@ -205,6 +276,8 @@
 
     lax.fori_loop(0, facets, add_facet, 0)
     inv[...] = 1.0 / jnp.maximum(inv[...], 0.5)
+    hear(0, (z > 1) & high)
+    hear(1, (z < levels - 2) & low)
 
     def gather_x(d, c):
         total = blocks[d, x, span(c)]
@@ -215,45 +288,35 @@
 
     def pass_early(t):
         d = dest(t)
-        right = d > z
-        way = jnp.where(right, 0, 1)
-        target = jnp.where(right, z + 1, z - 1)
-        fed = jnp.where(right, z > 0, z < levels - 1)
-
-        @pl.when(fed)
+        target, slot = route(d)
+
+        @pl.when(is_fed(t))
         def _():
-            f_copy(way, d, target).wait_recv()
-            fsend[d] += frecv[way, d]
-            f_copy(way, d, target).start()
+            f_copy(d, z, inlet(d)).wait_recv()
+            fsend[d] = blocks[d, :, pl.ds(0, early)] + frecv[inlet(d)]
+            f_copy(d, target, slot).start()
 
     def pass_rest(t):
         d = dest(t)
-        right = d > z
-        way = jnp.where(right, 0, 1)
-        target = jnp.where(right, z + 1, z - 1)
-        fed = jnp.where(right, z > 0, z < levels - 1)
+        target, slot = route(d)
         for c in range(len(chunks)):
             zsend[d, span(c)] = gather_x(d, c)
 
-            @pl.when(fed)
-            def _():
-                z_copy(way, d, c, target).wait_recv()
-                zsend[d, span(c)] += zrecv[way, d, span(c)]
-
-            z_copy(way, d, c, target).start()
+            @pl.when(is_fed(t))
+            def _():
+                z_copy(d, c, z, inlet(d)).wait_recv()
+                zsend[d, span(c)] += zrecv[inlet(d), span(c)]
+
+            z_copy(d, c, target, slot).start()
 
     def swap_early():
         fkeep[...] = blocks[z, :, pl.ds(0, early)]
-
-        @pl.when(z > 0)
-        def _():
-            f_copy(0, z, z - 1).wait_recv()
-            fkeep[...] += frecv[0, z]
-
-        @pl.when(z < levels - 1)
-        def _():
-            f_copy(1, z, z + 1).wait_recv()
-            fkeep[...] += frecv[1, z]
+        for level, there in sources():
+
+            @pl.when(there)
+            def _():
+                f_copy(z, z, level).wait_recv()
+                fkeep[...] += frecv[level]
 
         for k in range(1, lanes):
             fxsend[k - 1] = fkeep[lane_of(k)]
@@ -270,29 +333,28 @@
             p_copy(k, i).start()
 
     for t in range(levels - 1):
+        pass_rest(t)
         if t == 0:
-            pass_early(0)
-        if t == min(1, levels - 2):
-            for later in range(1, levels - 1):
-                pass_early(later)
-        if t == levels - 2:
-            swap_early()
-        pass_rest(t)
+            for u in range(levels - 1):
+                pass_early(u)
+    swap_early()
+    hear(0, (z > 0) & jnp.logical_not(high) & (levels > 1))
+    hear(1, (z < levels - 1) & jnp.logical_not(low) & (levels > 1))
 
     for c in range(len(chunks)):
-        zsend[z, span(c)] = gather_x(z, c)
-
-        @pl.when(z > 0)
-        def _():
-            z_copy(0, z, c, z - 1).wait_recv()
-            zsend[z, span(c)] += zrecv[0, z, span(c)]
-
-        @pl.when(z < levels - 1)
-        def _():
-            z_copy(1, z, c, z + 1).wait_recv()
-            zsend[z, span(c)] += zrecv[1, z, span(c)]
-
-        settle(1 + c, zsend[z, span(c)])
+        zsend[z, span(c)] = blocks[z, x, span(c)]
+        for level, there in sources():
+
+            @pl.when(there)
+            def _():
+                z_copy(z, c, z, level).wait_recv()
+                zsend[z, span(c)] += zrecv[level, span(c)]
+
+        total = zsend[z, span(c)]
+        for k in range(1, lanes):
+            x_copy(k, z, c).wait_recv()
+            total = total + xrecv[k - 1, z, span(c)]
+        settle(1 + c, total)
     total = fkeep[x]
     for k in range(1, lanes):
         g_copy(k).wait_recv()
@@ -315,15 +377,14 @@
     for k in range(1, lanes):
         g_copy(k).wait_send()
     for t in range(levels):
-        d = dest(t)
-        target = jnp.where(d > z, z + 1, z - 1)
+        d = dest(t) if t < levels - 1 else z
         for c in range(len(chunks)):
             for k in range(1, lanes):
                 x_copy(k, d, c).wait_send()
             if t < levels - 1:
-                z_copy(0, d, c, target).wait_send()
+                z_copy(d, c, z, z).wait_send()
         if t < levels - 1:
-            f_copy(0, d, target).wait_send()
+            f_copy(d, z, z).wait_send()
 
 
 def finish(stitched_ref, power_ref, out_ref, power_out, sems):
@@ -342,7 +403,6 @@
     height = fh // 4
     levels = strips // lanes
     others = max(lanes - 1, 1)
-    smem = pl.BlockSpec(memory_space=pltpu.SMEM)
     vmem = pl.BlockSpec(memory_space=pltpu.VMEM)
     hbm = pl.BlockSpec(memory_space=pltpu.HBM)
     dma = pltpu.SemaphoreType.DMA
@@ -351,16 +411,17 @@
     chunks = len(column_chunks(tiles, early))
     block_bytes = 4 * height * fw
     margin = 4 * 1024 * 1024
-    blocks = 8 * local + (2 + others) * strips + 4 * levels + 4
+    blocks = 8 * local + (2 + others) * strips + 5 * levels + 4
     stitched, power = pl.pallas_call(
         functools.partial(kernel, strips, lanes),
         out_shape=(
             jax.ShapeDtypeStruct((height, fw), jnp.float32),
             jax.ShapeDtypeStruct((tiles, TILE), jnp.float32),
         ),
-        in_specs=[smem] * 5 + [hbm] * 3,
+        in_specs=[hbm] * 8,
         out_specs=(vmem, vmem),
-        scratch_shapes=[
+        scratch_shapes=[pltpu.SMEM(slots.shape, jnp.int32)] * 5
+        + [
             pltpu.VMEM((local, fh, fw), jnp.float32),
             pltpu.VMEM((1, fh), jnp.float32),
             pltpu.VMEM((tiles, TILE), jnp.float32),
@@ -369,21 +430,22 @@
             pltpu.VMEM((tiles, height, TILE), jnp.float32),
             pltpu.VMEM((others, levels, tiles, height, TILE), jnp.float32),
             pltpu.VMEM((levels, tiles, height, TILE), jnp.float32),
-            pltpu.VMEM((2, levels, tiles, height, TILE), jnp.float32),
+            pltpu.VMEM((3 * levels, tiles, height, TILE), jnp.float32),
             pltpu.VMEM((levels, lanes, early, height, TILE), jnp.float32),
-            pltpu.VMEM((2, levels, lanes, early, height, TILE), jnp.float32),
+            pltpu.VMEM((3 * levels, lanes, early, height, TILE), jnp.float32),
             pltpu.VMEM((lanes, early, height, TILE), jnp.float32),
             pltpu.VMEM((others, early, height, TILE), jnp.float32),
             pltpu.VMEM((others, early, height, TILE), jnp.float32),
             pltpu.VMEM((tiles, 1, TILE), jnp.float32),
             pltpu.VMEM((strips - 1, tiles, 1, TILE), jnp.float32),
-            dma((2 + local,)),
+            pltpu.SemaphoreType.REGULAR((2,)),
+            dma((7 + local,)),
             dma((others, levels, chunks)),
             dma((others, levels, chunks)),
             dma((levels, chunks)),
-            dma((2, levels, chunks)),
+            dma((3 * levels, chunks)),
             dma((levels,)),
-            dma((2, levels)),
+            dma((3 * levels,)),
             dma((others,)),
             dma((others,)),
             dma((strips - 1, chunks + 1)),

time: 30.2 us -> 27.6 us (0.914)
  Pallas kernels: 29.4 us -> 26.8 us
    pallas_call x1, Pallas kernels: 28.7 us -> 26.1 us  [body(): pl.pallas_call(functools.partial(kernel, strips, lanes), out_shape=(jax.S...]
where the time goes in v2:
time: 27.6 us; the launch traced here: 27.4 us
  Pallas kernels  26.8 us (97%)
  between operations  0.64 us (2%)
    pallas_call x1, Pallas kernels, body(): pl.pallas_call(functools.partial(kernel, strips, lanes), out_shape=(jax.S...  26.1 us
    pallas_call x1, Pallas kernels, body(): pl.pallas_call(finish, out_shape=(jax.ShapeDtypeStruct((height, fw), jnp....  0.69 us

profile of v2, /device:TPU:0, one launch (start us, length us, event | category | flops | bytes accessed | tf_op | source)
XLA Modules:
  0.0 27.4 jit_solution(1969912340316791780)
XLA Ops:
  0.6 26.1 %shard_map.95 = (f32[16,2560]{1,0:T(8,128)S(1)}, f32[20,128]{1,0:T(8,128)S(1)}) custom-call(s32[16]{0:T(128)} %slots_hbm.1, s32[16]{0:T(128)} %row_hbm.1, s32[16]{0:T(128)} %col_hbm.1, s32[16]{0:T(128)} %first_hbm.1, s32[16]{0:T(128)} %end_hbm.1, f32[1,64]{1,0:T(1,128)} %bitcast.4, f32[20,128]{1,0:T(8,128)} %bitcast.3, f32[2,64,2560]{2,1,0:T(8,128)} %res_hbm.1), custom_call_target="tpu_custom_call" | custom-call | tf_op jit(solution)/shard_map/pallas_call | solution.py:415
  26.8 0.7 %shard_map.96 = (f32[16,2560]{1,0:T(8,128)}, f32[20,128]{1,0:T(8,128)}) custom-call(f32[16,2560]{1,0:T(8,128)S(1)} %get-tuple-element.6.stitched_ref, f32[20,128]{1,0:T(8,128)S(1)} %get-tuple-element.7.power_ref), custom_call_target="tpu_custom_call" | custom-call | tf_op jit(solution)/shard_map/pallas_call | solution.py:466

commit v3 on v2

--- a/solution.py
+++ b/solution.py
@@ -9,7 +9,7 @@
 from jax.sharding import PartitionSpec as P
 
 MESH = pl.DeviceIdType.MESH
-CHUNKS = 4
+CHUNKS = 3
 EARLY = 0.15
 TILE = 128
 
@@ -44,7 +44,7 @@
     strips, lanes,
     slots_hbm, row_hbm, col_hbm, first_hbm, end_hbm, rows_hbm, cols_hbm, res_hbm,
     out_ref, power_ref,
-    slots_ref, row_ref, col_ref, first_ref, end_ref, res_ref, rows_ref, cols_ref, rolled, blocks, inv, xrecv, zsend, zrecv,
+    slots_ref, row_ref, col_ref, first_ref, end_ref, res_ref, rows_ref, cols_ref, turned, blocks, inv, xrecv, zsend, zrecv,
     fsend, frecv, fkeep, fxsend, fxrecv, psend, precv,
     line, in_sem, xs_sem, xr_sem, zs_sem, zr_sem, fs_sem, fr_sem, gs_sem, gr_sem, ps_sem, pr_sem,
 ):
@@ -199,35 +199,56 @@
     u = lax.broadcasted_iota(jnp.int32, (1, fw), 1)
     row_taper = taper(y, fh)
     col_taper = taper(u, fw)
+    lane = lax.broadcasted_iota(jnp.int32, (fh, TILE), 1)
+    sub = lax.broadcasted_iota(jnp.int32, (8, TILE), 0)
+    blank = jnp.zeros((fh, TILE), jnp.float32)
+    for p in range(local):
+        for i in range(tiles + 1):
+            turned[p, i] = blank
+            turned[p, 2 * tiles + 1 + i] = blank
     for load in loads[:small]:
         load.wait()
     corr_row = jnp.sum(jnp.where(eye, rows_ref[...], 0.0), axis=1, keepdims=True)
     corr_col = jnp.concatenate([cols_ref[pl.ds(i, 1), :] for i in range(tiles)], axis=1)
     col_scale = col_taper * corr_col
-    anchors = []
+    spots = []
     for p in range(local):
         f = slots_ref[strip * local + p]
         ra, ca = row_ref[f], col_ref[f]
-        anchors.append(ra)
         inside = (y >= first_ref[f]) & (y < end_ref[f])
-        row_scale = jnp.where(inside, row_taper, 0.0) * corr_row
-        col_pos = u + (group * fw - ca)
-        col_inside = (col_pos >= 0) & (col_pos < fw)
-        shift = lax.rem(ca, fw)
+        row_scale = jnp.broadcast_to(jnp.where(inside, row_taper, 0.0) * corr_row, (fh, TILE))
+        turn = ca & (TILE - 1)
+        base = jnp.clip(group * tiles - (ca >> 7), -tiles, tiles + 1) + tiles + 1
+        spots.append((ra & 7, ra >> 3, turn, base))
         loads[small + p].wait()
-        for row in range(0, fh, 8):
-            term = res_ref[p, pl.ds(row, 8), :] * col_scale * row_scale[row : row + 8]
-            rolled[p, pl.ds(row, 8), :] = jnp.where(col_inside, pltpu.roll(term, shift, axis=1), 0.0)
-    spare = jnp.zeros((strips * height - fh, TILE), jnp.float32)
+        for i in range(tiles):
+            columns = pl.ds(i * TILE, TILE)
+            term = res_ref[p, :, columns] * col_scale[:, i * TILE : (i + 1) * TILE] * row_scale
+            turned[p, tiles + 1 + i] = pltpu.roll(term, turn, axis=1)
 
     def place(j):
-        total = None
+        bands = strips * height // 8
+        total = [None] * bands
         for p in range(local):
-            piece = jnp.concatenate([rolled[p, :, pl.ds(j * TILE, TILE)], spare], axis=0)
-            piece = pltpu.roll(piece, anchors[p], axis=0)
-            total = piece if total is None else total + piece
+            lift, drop, turn, base = spots[p]
+            piece = jnp.where(lane < turn, turned[p, base + (j - 1)], turned[p, base + j])
+            zero = jnp.zeros((8, TILE), jnp.float32)
+            rows, held = [], zero
+            for row in range(0, fh, 8):
+                band = pltpu.roll(piece[row : row + 8], lift, axis=0)
+                rows.append(jnp.where(sub < lift, held, band))
+                held = band
+            rows.append(jnp.where(sub < lift, held, 0.0))
+            step = 1
+            while step <= bands - fh // 8:
+                rows = rows + [zero] * min(step, bands - len(rows))
+                moved = [zero] * min(step, bands) + rows
+                rows = [jnp.where((drop & step) != 0, new, old) for new, old in zip(moved, rows)]
+                step *= 2
+            total = [band if old is None else old + band for old, band in zip(total, rows)]
         for s in range(strips):
-            blocks[s // lanes, s % lanes, j] = total[s * height : (s + 1) * height]
+            for i in range(height // 8):
+                blocks[s // lanes, s % lanes, j, pl.ds(i * 8, 8), :] = total[s * (height // 8) + i]
 
     def open_early():
         for t in range(levels - 1):
@@ -363,16 +384,6 @@
 
     for i in range(len(parts)):
         for k in range(1, strips):
-            p_copy(k, i).wait_recv()
-    total = psend[...]
-    for k in range(1, strips):
-        total = total + precv[k - 1]
-    total = total * (1.0 / (strips * height))
-    for j in range(tiles):
-        power_ref[pl.ds(j, 1), :] = total[j]
-
-    for i in range(len(parts)):
-        for k in range(1, strips):
             p_copy(k, i).wait_send()
     for k in range(1, lanes):
         g_copy(k).wait_send()
@@ -385,6 +396,16 @@
                 z_copy(d, c, z, z).wait_send()
         if t < levels - 1:
             f_copy(d, z, z).wait_send()
+
+    for i in range(len(parts)):
+        for k in range(1, strips):
+            p_copy(k, i).wait_recv()
+    total = psend[...]
+    for k in range(1, strips):
+        total = total + precv[k - 1]
+    total = total * (1.0 / (strips * height))
+    for j in range(tiles):
+        power_ref[pl.ds(j, 1), :] = total[j]
 
 
 def finish(stitched_ref, power_ref, out_ref, power_out, sems):
@@ -411,7 +432,7 @@
     chunks = len(column_chunks(tiles, early))
     block_bytes = 4 * height * fw
     margin = 4 * 1024 * 1024
-    blocks = 8 * local + (2 + others) * strips + 5 * levels + 4
+    blocks = 18 * local + (2 + others) * strips + 5 * levels + 4
     stitched, power = pl.pallas_call(
         functools.partial(kernel, strips, lanes),
         out_shape=(
@@ -425,7 +446,7 @@
             pltpu.VMEM((local, fh, fw), jnp.float32),
             pltpu.VMEM((1, fh), jnp.float32),
             pltpu.VMEM((tiles, TILE), jnp.float32),
-            pltpu.VMEM((local, fh, fw), jnp.float32),
+            pltpu.VMEM((local, 3 * tiles + 2, fh, TILE), jnp.float32),
             pltpu.VMEM((levels, lanes, tiles, height, TILE), jnp.float32),
             pltpu.VMEM((tiles, height, TILE), jnp.float32),
             pltpu.VMEM((others, levels, tiles, height, TILE), jnp.float32),

time: 27.6 us -> 26.8 us (0.971)
  Pallas kernels: 26.8 us -> 26 us
    pallas_call x1, Pallas kernels: 26.1 us -> 25.3 us  [body(): pl.pallas_call(functools.partial(kernel, strips, lanes), out_shape=(jax.S...]
where the time goes in v3:
time: 26.8 us; the launch traced here: 26.6 us
  Pallas kernels  26 us (97%)
  between operations  0.64 us (2%)
    pallas_call x1, Pallas kernels, body(): pl.pallas_call(functools.partial(kernel, strips, lanes), out_shape=(jax.S...  25.3 us
    pallas_call x1, Pallas kernels, body(): pl.pallas_call(finish, out_shape=(jax.ShapeDtypeStruct((height, fw), jnp....  0.69 us

profile of v3, /device:TPU:0, one launch (start us, length us, event | category | flops | bytes accessed | tf_op | source)
XLA Modules:
  0.0 26.6 jit_solution(9591421630292696301)
XLA Ops:
  0.6 25.3 %shard_map.95 = (f32[16,2560]{1,0:T(8,128)S(1)}, f32[20,128]{1,0:T(8,128)S(1)}) custom-call(s32[16]{0:T(128)} %slots_hbm.1, s32[16]{0:T(128)} %row_hbm.1, s32[16]{0:T(128)} %col_hbm.1, s32[16]{0:T(128)} %first_hbm.1, s32[16]{0:T(128)} %end_hbm.1, f32[1,64]{1,0:T(1,128)} %bitcast.4, f32[20,128]{1,0:T(8,128)} %bitcast.3, f32[2,64,2560]{2,1,0:T(8,128)} %res_hbm.1), custom_call_target="tpu_custom_call" | custom-call | tf_op jit(solution)/shard_map/pallas_call | solution.py:436
  26.0 0.7 %shard_map.96 = (f32[16,2560]{1,0:T(8,128)}, f32[20,128]{1,0:T(8,128)}) custom-call(f32[16,2560]{1,0:T(8,128)S(1)} %get-tuple-element.6.stitched_ref, f32[20,128]{1,0:T(8,128)S(1)} %get-tuple-element.7.power_ref), custom_call_target="tpu_custom_call" | custom-call | tf_op jit(solution)/shard_map/pallas_call | solution.py:487

commit v4 on v3

--- a/solution.py
+++ b/solution.py
@@ -9,7 +9,7 @@
 from jax.sharding import PartitionSpec as P
 
 MESH = pl.DeviceIdType.MESH
-CHUNKS = 3
+SHARES = (5, 6, 6)
 EARLY = 0.15
 TILE = 128
 
@@ -35,8 +35,24 @@
     ]
 
 
+def inlets(levels):
+    def inner(level):
+        return 0 < level < levels - 1
+
+    tables = []
+    for z in range(levels):
+        passed = [("pass", d) for d in range(levels) if d != z and fed(levels, z, d)]
+        direct = [
+            ("sum", s) for s in range(levels)
+            if s != z and (inner(s) or (z == (1 if s == 0 else levels - 2)))
+        ]
+        tables.append(passed + direct)
+    return tables
+
+
 def column_chunks(tiles, first):
-    edges = [first + (tiles - first) * c // CHUNKS for c in range(CHUNKS + 1)]
+    ends = [sum(SHARES[:c]) for c in range(len(SHARES) + 1)]
+    edges = [first + (tiles - first) * end // ends[-1] for end in ends]
     return [(a, b - a) for a, b in zip(edges, edges[1:]) if b > a]
 
 
@@ -46,7 +62,7 @@
     out_ref, power_ref,
     slots_ref, row_ref, col_ref, first_ref, end_ref, res_ref, rows_ref, cols_ref, turned, blocks, inv, xrecv, zsend, zrecv,
     fsend, frecv, fkeep, fxsend, fxrecv, psend, precv,
-    line, in_sem, xs_sem, xr_sem, zs_sem, zr_sem, fs_sem, fr_sem, gs_sem, gr_sem, ps_sem, pr_sem,
+    line, in_sem, sent, xr_sem, zr_sem, fr_sem, gr_sem, pr_sem,
 ):
     local, fh, fw = res_ref.shape
     facets = slots_ref.shape[0]
@@ -121,20 +137,29 @@
     def is_fed(t):
         return pick([int(fed(levels, level, row[t])) for level, row in enumerate(order)]) == 1
 
-    def route(d):
-        target = jnp.where(z == 0, min(1, levels - 1), jnp.where(high, d, levels - 2))
-        slot = jnp.where(target == d, z, jnp.where(z == 0, levels + d, 2 * levels + d))
-        return target, slot
-
-    def inlet(d):
-        return jnp.where(d > z, levels + d, 2 * levels + d)
+    tables = inlets(levels)
+    leaves = {0: min(1, levels - 1), levels - 1: max(levels - 2, 0)}
+
+    def route(t):
+        targets, slots = [], []
+        for level, row in enumerate(order):
+            target = leaves.get(level, row[t])
+            kind = ("sum", level) if target == row[t] else ("pass", row[t])
+            targets.append(target)
+            slots.append(tables[target].index(kind))
+        return pick(targets), pick(slots)
+
+    def inlet(t):
+        return pick([
+            tables[level].index(("pass", row[t])) if fed(levels, level, row[t]) else 0
+            for level, row in enumerate(order)
+        ])
 
     def sources():
-        for level in range(levels):
-            if 0 < level < levels - 1:
-                yield level, z != level
-            elif levels > 1:
-                yield level, z == (1 if level == 0 else levels - 2)
+        for i in range(max(len(table) for table in tables)):
+            which = [i < len(table) and table[i][0] == "sum" for table in tables]
+            if any(which):
+                yield i, pick([int(there) for there in which]) == 1
 
     def lane_of(k):
         return lax.rem(x + k, lanes)
@@ -146,7 +171,7 @@
         return pltpu.make_async_remote_copy(
             src_ref=blocks.at[d, lane_of(k), span(c)],
             dst_ref=xrecv.at[k - 1, d, span(c)],
-            send_sem=xs_sem.at[k - 1, d, c],
+            send_sem=sent.at[0],
             recv_sem=xr_sem.at[k - 1, d, c],
             device_id=at(z, lane_of(k)),
             device_id_type=MESH,
@@ -156,7 +181,7 @@
         return pltpu.make_async_remote_copy(
             src_ref=zsend.at[d, span(c)],
             dst_ref=zrecv.at[slot, span(c)],
-            send_sem=zs_sem.at[d, c],
+            send_sem=sent.at[1],
             recv_sem=zr_sem.at[slot, c],
             device_id=at(target, x),
             device_id_type=MESH,
@@ -166,7 +191,7 @@
         return pltpu.make_async_remote_copy(
             src_ref=fsend.at[d] if source is None else source,
             dst_ref=frecv.at[slot],
-            send_sem=fs_sem.at[d],
+            send_sem=sent.at[2],
             recv_sem=fr_sem.at[slot],
             device_id=at(target, x),
             device_id_type=MESH,
@@ -176,7 +201,7 @@
         return pltpu.make_async_remote_copy(
             src_ref=fxsend.at[k - 1],
             dst_ref=fxrecv.at[k - 1],
-            send_sem=gs_sem.at[k - 1],
+            send_sem=sent.at[3],
             recv_sem=gr_sem.at[k - 1],
             device_id=at(z, lane_of(k)),
             device_id_type=MESH,
@@ -186,8 +211,8 @@
         return pltpu.make_async_remote_copy(
             src_ref=psend.at[pl.ds(*parts[i])],
             dst_ref=precv.at[k - 1, pl.ds(*parts[i])],
-            send_sem=ps_sem.at[k - 1, i],
-            recv_sem=pr_sem.at[k - 1, i],
+            send_sem=sent.at[4],
+            recv_sem=pr_sem.at[i],
             device_id={"strip": lax.rem(strip + k, strips)},
             device_id_type=MESH,
         )
@@ -253,27 +278,37 @@
     def open_early():
         for t in range(levels - 1):
             d = dest(t)
-            target, slot = route(d)
+            target, slot = route(t)
 
             @pl.when(jnp.logical_not(is_fed(t)))
             def _():
                 f_copy(d, target, slot, blocks.at[d, :, pl.ds(0, early)]).start()
 
-    for i, (first, count) in enumerate(parts):
+    def open_chunk(c):
+        @pl.when(lax.rem(group, 2) == 0)
+        def _():
+            for k in range(1, lanes):
+                x_copy(k, dest(0), c).start()
+
+    openers = [lambda: open_chunk(0), open_early] + [
+        functools.partial(open_chunk, c) for c in range(1, len(chunks))
+    ]
+    for i, (first, count) in enumerate([chunks[0], parts[0]] + chunks[1:]):
         for j in range(first, first + count):
             place(j)
             if j == first and i == 1:
                 enter()
-                open_early()
-            if j == first and i > 1:
+            if j == first and i > 0:
+                openers[i - 1]()
+    openers[-1]()
+
+    @pl.when(lax.rem(group, 2) == 0)
+    def _():
+        for t in range(1, levels):
+            for c in range(len(chunks)):
                 for k in range(1, lanes):
-                    x_copy(k, dest(0), i - 2).start()
-    for k in range(1, lanes):
-        x_copy(k, dest(0), len(chunks) - 1).start()
-    for t in range(1, levels):
-        for c in range(len(chunks)):
-            for k in range(1, lanes):
-                x_copy(k, dest(t) if t < levels - 1 else z, c).start()
+                    x_copy(k, dest(t) if t < levels - 1 else z, c).start()
+
     hear(0, (z == 1) & high)
     hear(1, (z == levels - 2) & low)
 
@@ -297,6 +332,14 @@
 
     lax.fori_loop(0, facets, add_facet, 0)
     inv[...] = 1.0 / jnp.maximum(inv[...], 0.5)
+
+    @pl.when(lax.rem(group, 2) == 1)
+    def _():
+        for t in range(0, levels):
+            for c in range(len(chunks)):
+                for k in range(1, lanes):
+                    x_copy(k, dest(t) if t < levels - 1 else z, c).start()
+
     hear(0, (z > 1) & high)
     hear(1, (z < levels - 2) & low)
 
@@ -309,24 +352,24 @@
 
     def pass_early(t):
         d = dest(t)
-        target, slot = route(d)
+        target, slot = route(t)
 
         @pl.when(is_fed(t))
         def _():
-            f_copy(d, z, inlet(d)).wait_recv()
-            fsend[d] = blocks[d, :, pl.ds(0, early)] + frecv[inlet(d)]
+            f_copy(d, z, inlet(t)).wait_recv()
+            fsend[d] = blocks[d, :, pl.ds(0, early)] + frecv[inlet(t)]
             f_copy(d, target, slot).start()
 
     def pass_rest(t):
         d = dest(t)
-        target, slot = route(d)
+        target, slot = route(t)
         for c in range(len(chunks)):
             zsend[d, span(c)] = gather_x(d, c)
 
             @pl.when(is_fed(t))
             def _():
-                z_copy(d, c, z, inlet(d)).wait_recv()
-                zsend[d, span(c)] += zrecv[inlet(d), span(c)]
+                z_copy(d, c, z, inlet(t)).wait_recv()
+                zsend[d, span(c)] += zrecv[inlet(t), span(c)]
 
             z_copy(d, c, target, slot).start()
 
@@ -382,30 +425,36 @@
         total = total + fxrecv[k - 1]
     settle(0, total)
 
-    for i in range(len(parts)):
+    def drain(i, ref):
+        pltpu.make_async_remote_copy(
+            src_ref=ref, dst_ref=ref, send_sem=sent.at[i], recv_sem=sent.at[i],
+            device_id=at(z, x), device_id_type=MESH,
+        ).wait_send()
+
+    rest = pl.ds(early, tiles - early)
+    if lanes > 1:
+        drain(0, xrecv.at[:, :, rest])
+        drain(3, fxsend)
+    if levels > 1:
+        drain(1, zsend.at[pl.ds(0, levels - 1), rest])
+        drain(2, fsend.at[pl.ds(0, levels - 1)])
+    if strips > 1:
+        drain(4, precv)
+
+    for i in list(range(1, len(parts))) + [0]:
+        first, count = parts[i]
+        if strips > 1:
+            came = precv.at[:, pl.ds(first, count)]
+            pltpu.make_async_remote_copy(
+                src_ref=came, dst_ref=came, send_sem=sent.at[4], recv_sem=pr_sem.at[i],
+                device_id=at(z, x), device_id_type=MESH,
+            ).wait_recv()
+        total = psend[pl.ds(first, count)]
         for k in range(1, strips):
-            p_copy(k, i).wait_send()
-    for k in range(1, lanes):
-        g_copy(k).wait_send()
-    for t in range(levels):
-        d = dest(t) if t < levels - 1 else z
-        for c in range(len(chunks)):
-            for k in range(1, lanes):
-                x_copy(k, d, c).wait_send()
-            if t < levels - 1:
-                z_copy(d, c, z, z).wait_send()
-        if t < levels - 1:
-            f_copy(d, z, z).wait_send()
-
-    for i in range(len(parts)):
-        for k in range(1, strips):
-            p_copy(k, i).wait_recv()
-    total = psend[...]
-    for k in range(1, strips):
-        total = total + precv[k - 1]
-    total = total * (1.0 / (strips * height))
-    for j in range(tiles):
-        power_ref[pl.ds(j, 1), :] = total[j]
+            total = total + precv[k - 1, pl.ds(first, count)]
+        total = total * (1.0 / (strips * height))
+        for j in range(count):
+            power_ref[pl.ds(first + j, 1), :] = total[j]
 
 
 def finish(stitched_ref, power_ref, out_ref, power_out, sems):
@@ -430,6 +479,7 @@
     tiles = fw // TILE
     early = max(round(EARLY * tiles), 1)
     chunks = len(column_chunks(tiles, early))
+    slots_in = max([len(table) for table in inlets(levels)] + [1])
     block_bytes = 4 * height * fw
     margin = 4 * 1024 * 1024
     blocks = 18 * local + (2 + others) * strips + 5 * levels + 4
@@ -451,9 +501,9 @@
             pltpu.VMEM((tiles, height, TILE), jnp.float32),
             pltpu.VMEM((others, levels, tiles, height, TILE), jnp.float32),
             pltpu.VMEM((levels, tiles, height, TILE), jnp.float32),
-            pltpu.VMEM((3 * levels, tiles, height, TILE), jnp.float32),
+            pltpu.VMEM((slots_in, tiles, height, TILE), jnp.float32),
             pltpu.VMEM((levels, lanes, early, height, TILE), jnp.float32),
-            pltpu.VMEM((3 * levels, lanes, early, height, TILE), jnp.float32),
+            pltpu.VMEM((slots_in, lanes, early, height, TILE), jnp.float32),
             pltpu.VMEM((lanes, early, height, TILE), jnp.float32),
             pltpu.VMEM((others, early, height, TILE), jnp.float32),
             pltpu.VMEM((others, early, height, TILE), jnp.float32),
@@ -461,16 +511,12 @@
             pltpu.VMEM((strips - 1, tiles, 1, TILE), jnp.float32),
             pltpu.SemaphoreType.REGULAR((2,)),
             dma((7 + local,)),
+            dma((5,)),
             dma((others, levels, chunks)),
-            dma((others, levels, chunks)),
-            dma((levels, chunks)),
-            dma((3 * levels, chunks)),
-            dma((levels,)),
-            dma((3 * levels,)),
+            dma((slots_in, chunks)),
+            dma((slots_in,)),
             dma((others,)),
-            dma((others,)),
-            dma((strips - 1, chunks + 1)),
-            dma((strips - 1, chunks + 1)),
+            dma((chunks + 1,)),
         ],
         compiler_params=pltpu.CompilerParams(
             collective_id=0,

time: 26.8 us -> 25 us (0.933)
  Pallas kernels: 26 us -> 24.2 us
    pallas_call x1, Pallas kernels: 25.3 us -> 23.5 us  [body(): pl.pallas_call(functools.partial(kernel, strips, lanes), out_shape=(jax.S...]
where the time goes in v4:
time: 25 us; the launch traced here: 24.8 us
  Pallas kernels  24.2 us (97%)
  between operations  0.64 us (3%)
    pallas_call x1, Pallas kernels, body(): pl.pallas_call(functools.partial(kernel, strips, lanes), out_shape=(jax.S...  23.5 us
    pallas_call x1, Pallas kernels, body(): pl.pallas_call(finish, out_shape=(jax.ShapeDtypeStruct((height, fw), jnp....  0.69 us

profile of v4, /device:TPU:0, one launch (start us, length us, event | category | flops | bytes accessed | tf_op | source)
XLA Modules:
  0.0 24.8 jit_solution(2130902223471778397)
XLA Ops:
  0.6 23.5 %shard_map.95 = (f32[16,2560]{1,0:T(8,128)S(1)}, f32[20,128]{1,0:T(8,128)S(1)}) custom-call(s32[16]{0:T(128)} %slots_hbm.1, s32[16]{0:T(128)} %row_hbm.1, s32[16]{0:T(128)} %col_hbm.1, s32[16]{0:T(128)} %first_hbm.1, s32[16]{0:T(128)} %end_hbm.1, f32[1,64]{1,0:T(1,128)} %bitcast.4, f32[20,128]{1,0:T(8,128)} %bitcast.3, f32[2,64,2560]{2,1,0:T(8,128)} %res_hbm.1), custom_call_target="tpu_custom_call" | custom-call | tf_op jit(solution)/shard_map/pallas_call | solution.py:486
  24.2 0.7 %shard_map.96 = (f32[16,2560]{1,0:T(8,128)}, f32[20,128]{1,0:T(8,128)}) custom-call(f32[16,2560]{1,0:T(8,128)S(1)} %get-tuple-element.6.stitched_ref, f32[20,128]{1,0:T(8,128)S(1)} %get-tuple-element.7.power_ref), custom_call_target="tpu_custom_call" | custom-call | tf_op jit(solution)/shard_map/pallas_call | solution.py:533

commit v5 on v4

--- a/solution.py
+++ b/solution.py
@@ -60,11 +60,11 @@
     strips, lanes,
     slots_hbm, row_hbm, col_hbm, first_hbm, end_hbm, rows_hbm, cols_hbm, res_hbm,
     out_ref, power_ref,
-    slots_ref, row_ref, col_ref, first_ref, end_ref, res_ref, rows_ref, cols_ref, turned, blocks, inv, xrecv, zsend, zrecv,
+    slots_ref, row_ref, col_ref, first_ref, end_ref, rows_ref, cols_ref, scale, turned, blocks, inv, xrecv, zsend, zrecv,
     fsend, frecv, fkeep, fxsend, fxrecv, psend, precv,
-    line, in_sem, sent, xr_sem, zr_sem, fr_sem, gr_sem, pr_sem,
+    line, sent, xr_sem, zr_sem, fr_sem, gr_sem, pr_sem,
 ):
-    local, fh, fw = res_ref.shape
+    local, fh, fw = res_hbm.shape
     facets = slots_ref.shape[0]
     height = out_ref.shape[0]
     levels = strips // lanes
@@ -76,33 +76,37 @@
     group = lax.axis_index("col")
     z, x = lax.div(strip, lanes), lax.rem(strip, lanes)
 
+    low, high = z > 0, z < levels - 1
+    leaf = jnp.logical_not(low & high)
+
+    def at(level, lane):
+        return {"strip": level * lanes + lane}
+
+    barrier = pltpu.get_barrier_semaphore()
+    for k in range(1, lanes):
+        pl.semaphore_signal(barrier, device_id=at(z, lax.rem(x + k, lanes)), device_id_type=MESH)
+    for there, step in ((low, -1), (high, 1)):
+
+        @pl.when(there)
+        def _():
+            pl.semaphore_signal(barrier, device_id=at(z + step, x), device_id_type=MESH)
+
     sources = [
         (slots_hbm, slots_ref), (row_hbm, row_ref), (col_hbm, col_ref), (first_hbm, first_ref),
         (end_hbm, end_ref), (rows_hbm, rows_ref), (cols_hbm, cols_ref),
     ]
     small = len(sources)
-    sources += [(res_hbm.at[p], res_ref.at[p]) for p in range(local)]
     loads = [
-        pltpu.make_async_copy(source, target, in_sem.at[i])
+        pltpu.make_async_copy(source, target, sent.at[i])
         for i, (source, target) in enumerate(sources)
     ]
     for load in loads:
         load.start()
-
-    low, high = z > 0, z < levels - 1
-    leaf = jnp.logical_not(low & high)
-
-    def at(level, lane):
-        return {"strip": level * lanes + lane}
-
-    barrier = pltpu.get_barrier_semaphore()
-    for k in range(1, lanes):
-        pl.semaphore_signal(barrier, device_id=at(z, lax.rem(x + k, lanes)), device_id_type=MESH)
-    for there, step in ((low, -1), (high, 1)):
-
-        @pl.when(there)
-        def _():
-            pl.semaphore_signal(barrier, device_id=at(z + step, x), device_id_type=MESH)
+    for p in range(local):
+        for i in range(tiles):
+            pltpu.make_async_copy(
+                res_hbm.at[p, :, pl.ds(i * TILE, TILE)], turned.at[p, tiles + 1 + i], sent.at[small + p]
+            ).start()
 
     def enter():
         pl.semaphore_wait(barrier, lanes - 1 + low.astype(jnp.int32) + high.astype(jnp.int32))
@@ -231,11 +235,12 @@
         for i in range(tiles + 1):
             turned[p, i] = blank
             turned[p, 2 * tiles + 1 + i] = blank
-    for load in loads[:small]:
+    for load in loads:
         load.wait()
     corr_row = jnp.sum(jnp.where(eye, rows_ref[...], 0.0), axis=1, keepdims=True)
-    corr_col = jnp.concatenate([cols_ref[pl.ds(i, 1), :] for i in range(tiles)], axis=1)
-    col_scale = col_taper * corr_col
+    for i in range(tiles):
+        columns = slice(i * TILE, (i + 1) * TILE)
+        scale[i] = col_taper[:, columns] * cols_ref[pl.ds(i, 1), :]
     spots = []
     for p in range(local):
         f = slots_ref[strip * local + p]
@@ -244,23 +249,28 @@
         row_scale = jnp.broadcast_to(jnp.where(inside, row_taper, 0.0) * corr_row, (fh, TILE))
         turn = ca & (TILE - 1)
         base = jnp.clip(group * tiles - (ca >> 7), -tiles, tiles + 1) + tiles + 1
-        spots.append((ra & 7, ra >> 3, turn, base))
-        loads[small + p].wait()
-        for i in range(tiles):
-            columns = pl.ds(i * TILE, TILE)
-            term = res_ref[p, :, columns] * col_scale[:, i * TILE : (i + 1) * TILE] * row_scale
-            turned[p, tiles + 1 + i] = pltpu.roll(term, turn, axis=1)
+        spots.append((ra & 7, ra >> 3, turn, base, row_scale))
+    for p in range(local):
+        whole = turned.at[p, pl.ds(tiles + 1, tiles)]
+        pltpu.make_async_copy(whole, whole, sent.at[small + p]).wait()
 
     def place(j):
         bands = strips * height // 8
         total = [None] * bands
         for p in range(local):
-            lift, drop, turn, base = spots[p]
-            piece = jnp.where(lane < turn, turned[p, base + (j - 1)], turned[p, base + j])
+            lift, drop, turn, base, row_scale = spots[p]
+            spread = [
+                scale[jnp.clip(base + (i - tiles - 1), 0, tiles - 1)] for i in (j - 1, j)
+            ]
+            spread = pltpu.roll(
+                jnp.where(lane[:8] >= TILE - turn, *(jnp.broadcast_to(w, (8, TILE)) for w in spread)), turn, axis=1
+            )
+            piece = jnp.where(lane >= TILE - turn, turned[p, base + (j - 1)], turned[p, base + j])
+            piece = pltpu.roll(piece, turn, axis=1) * row_scale
             zero = jnp.zeros((8, TILE), jnp.float32)
             rows, held = [], zero
             for row in range(0, fh, 8):
-                band = pltpu.roll(piece[row : row + 8], lift, axis=0)
+                band = pltpu.roll(piece[row : row + 8] * spread, lift, axis=0)
                 rows.append(jnp.where(sub < lift, held, band))
                 held = band
             rows.append(jnp.where(sub < lift, held, 0.0))
@@ -482,7 +492,7 @@
     slots_in = max([len(table) for table in inlets(levels)] + [1])
     block_bytes = 4 * height * fw
     margin = 4 * 1024 * 1024
-    blocks = 18 * local + (2 + others) * strips + 5 * levels + 4
+    blocks = 14 * local + (2 + others) * strips + 5 * levels + 4
     stitched, power = pl.pallas_call(
         functools.partial(kernel, strips, lanes),
         out_shape=(
@@ -493,9 +503,9 @@
         out_specs=(vmem, vmem),
         scratch_shapes=[pltpu.SMEM(slots.shape, jnp.int32)] * 5
         + [
-            pltpu.VMEM((local, fh, fw), jnp.float32),
             pltpu.VMEM((1, fh), jnp.float32),
             pltpu.VMEM((tiles, TILE), jnp.float32),
+            pltpu.VMEM((tiles, 1, TILE), jnp.float32),
             pltpu.VMEM((local, 3 * tiles + 2, fh, TILE), jnp.float32),
             pltpu.VMEM((levels, lanes, tiles, height, TILE), jnp.float32),
             pltpu.VMEM((tiles, height, TILE), jnp.float32),
@@ -511,7 +521,6 @@
             pltpu.VMEM((strips - 1, tiles, 1, TILE), jnp.float32),
             pltpu.SemaphoreType.REGULAR((2,)),
             dma((7 + local,)),
-            dma((5,)),
             dma((others, levels, chunks)),
             dma((slots_in, chunks)),
             dma((slots_in,)),

time: 25 us -> 25 us (level)
  the two profiles are of different devices: /device:TPU:0 before, /device:TPU:1 now
where the time goes in v5:
time: 25 us; the launch traced here: 24.8 us
  Pallas kernels  24.1 us (96%)
  between operations  0.64 us (3%)
    pallas_call x1, Pallas kernels, body(): pl.pallas_call(functools.partial(kernel, strips, lanes), out_shape=(jax.S...  23.4 us
    pallas_call x1, Pallas kernels, body(): pl.pallas_call(finish, out_shape=(jax.ShapeDtypeStruct((height, fw), jnp....  0.69 us

profile of v5, /device:TPU:1, one launch (start us, length us, event | category | flops | bytes accessed | tf_op | source)
XLA Modules:
  0.0 24.8 jit_solution(1459196635773822937)
XLA Ops:
  0.6 23.4 %shard_map.95 = (f32[16,2560]{1,0:T(8,128)S(1)}, f32[20,128]{1,0:T(8,128)S(1)}) custom-call(s32[16]{0:T(128)} %slots_hbm.1, s32[16]{0:T(128)} %row_hbm.1, s32[16]{0:T(128)} %col_hbm.1, s32[16]{0:T(128)} %first_hbm.1, s32[16]{0:T(128)} %end_hbm.1, f32[1,64]{1,0:T(1,128)} %bitcast.4, f32[20,128]{1,0:T(8,128)} %bitcast.3, f32[2,64,2560]{2,1,0:T(8,128)} %res_hbm.1), custom_call_target="tpu_custom_call" | custom-call | tf_op jit(solution)/shard_map/pallas_call | solution.py:496
  24.1 0.7 %shard_map.96 = (f32[16,2560]{1,0:T(8,128)}, f32[20,128]{1,0:T(8,128)}) custom-call(f32[16,2560]{1,0:T(8,128)S(1)} %get-tuple-element.6.stitched_ref, f32[20,128]{1,0:T(8,128)S(1)} %get-tuple-element.7.power_ref), custom_call_target="tpu_custom_call" | custom-call | tf_op jit(solution)/shard_map/pallas_call | solution.py:542

commit v6 on v5

--- a/solution.py
+++ b/solution.py
@@ -9,7 +9,7 @@
 from jax.sharding import PartitionSpec as P
 
 MESH = pl.DeviceIdType.MESH
-SHARES = (5, 6, 6)
+SHARES = (4, 5, 4, 4)
 EARLY = 0.15
 TILE = 128
 
@@ -295,6 +295,11 @@
                 f_copy(d, target, slot, blocks.at[d, :, pl.ds(0, early)]).start()
 
     def open_chunk(c):
+        if c < 1:
+            for k in range(1, lanes):
+                x_copy(k, dest(0), c).start()
+            return
+
         @pl.when(lax.rem(group, 2) == 0)
         def _():
             for k in range(1, lanes):
@@ -346,7 +351,7 @@
     @pl.when(lax.rem(group, 2) == 1)
     def _():
         for t in range(0, levels):
-            for c in range(len(chunks)):
+            for c in range(1 if t == 0 else 0, len(chunks)):
                 for k in range(1, lanes):
                     x_copy(k, dest(t) if t < levels - 1 else z, c).start()
 

time: 25 us -> 24.8 us (level)
  the two profiles are of different devices: /device:TPU:1 before, /device:TPU:0 now
where the time goes in v6:
time: 24.8 us; the launch traced here: 24.5 us
  Pallas kernels  23.9 us (96%)
  between operations  0.64 us (3%)
    pallas_call x1, Pallas kernels, body(): pl.pallas_call(functools.partial(kernel, strips, lanes), out_shape=(jax.S...  23.2 us
    pallas_call x1, Pallas kernels, body(): pl.pallas_call(finish, out_shape=(jax.ShapeDtypeStruct((height, fw), jnp....  0.69 us

profile of v6, /device:TPU:0, one launch (start us, length us, event | category | flops | bytes accessed | tf_op | source)
XLA Modules:
  0.0 24.5 jit_solution(17601403391207895024)
XLA Ops:
  0.6 23.2 %shard_map.95 = (f32[16,2560]{1,0:T(8,128)S(1)}, f32[20,128]{1,0:T(8,128)S(1)}) custom-call(s32[16]{0:T(128)} %slots_hbm.1, s32[16]{0:T(128)} %row_hbm.1, s32[16]{0:T(128)} %col_hbm.1, s32[16]{0:T(128)} %first_hbm.1, s32[16]{0:T(128)} %end_hbm.1, f32[1,64]{1,0:T(1,128)} %bitcast.4, f32[20,128]{1,0:T(8,128)} %bitcast.3, f32[2,64,2560]{2,1,0:T(8,128)} %res_hbm.1), custom_call_target="tpu_custom_call" | custom-call | tf_op jit(solution)/shard_map/pallas_call | solution.py:501
  23.9 0.7 %shard_map.96 = (f32[16,2560]{1,0:T(8,128)}, f32[20,128]{1,0:T(8,128)}) custom-call(f32[16,2560]{1,0:T(8,128)S(1)} %get-tuple-element.6.stitched_ref, f32[20,128]{1,0:T(8,128)S(1)} %get-tuple-element.7.power_ref), custom_call_target="tpu_custom_call" | custom-call | tf_op jit(solution)/shard_map/pallas_call | solution.py:547

commit v7 on v6

--- a/solution.py
+++ b/solution.py
@@ -143,6 +143,16 @@
 
     tables = inlets(levels)
     leaves = {0: min(1, levels - 1), levels - 1: max(levels - 2, 0)}
+
+    beyond = [
+        [
+            level not in leaves and not fed(levels, level, d) and abs(d - level) > 1 for d in row
+        ]
+        for level, row in enumerate(order)
+    ]
+
+    def is_beyond(t):
+        return pick([int(row[t]) for row in beyond]) == 1
 
     def route(t):
         targets, slots = [], []
@@ -290,7 +300,11 @@
             d = dest(t)
             target, slot = route(t)
 
-            @pl.when(jnp.logical_not(is_fed(t)))
+            held = is_fed(t)
+            if any(row[t] for row in beyond):
+                held = held | is_beyond(t)
+
+            @pl.when(jnp.logical_not(held))
             def _():
                 f_copy(d, target, slot, blocks.at[d, :, pl.ds(0, early)]).start()
 
@@ -374,6 +388,12 @@
             f_copy(d, z, inlet(t)).wait_recv()
             fsend[d] = blocks[d, :, pl.ds(0, early)] + frecv[inlet(t)]
             f_copy(d, target, slot).start()
+
+        if any(row[t] for row in beyond):
+
+            @pl.when(is_beyond(t))
+            def _():
+                f_copy(d, target, slot, blocks.at[d, :, pl.ds(0, early)]).start()
 
     def pass_rest(t):
         d = dest(t)

time: 24.8 us -> 24.8 us (level)
  no operation moved by 1% of the time
where the time goes in v7:
time: 24.8 us; the launch traced here: 24.5 us
  Pallas kernels  23.9 us (96%)
  between operations  0.64 us (3%)
    pallas_call x1, Pallas kernels, body(): pl.pallas_call(functools.partial(kernel, strips, lanes), out_shape=(jax.S...  23.2 us
    pallas_call x1, Pallas kernels, body(): pl.pallas_call(finish, out_shape=(jax.ShapeDtypeStruct((height, fw), jnp....  0.69 us

profile of v7, /device:TPU:0, one launch (start us, length us, event | category | flops | bytes accessed | tf_op | source)
XLA Modules:
  0.0 24.5 jit_solution(17601403391207895024)
XLA Ops:
  0.6 23.2 %shard_map.95 = (f32[16,2560]{1,0:T(8,128)S(1)}, f32[20,128]{1,0:T(8,128)S(1)}) custom-call(s32[16]{0:T(128)} %slots_hbm.1, s32[16]{0:T(128)} %row_hbm.1, s32[16]{0:T(128)} %col_hbm.1, s32[16]{0:T(128)} %first_hbm.1, s32[16]{0:T(128)} %end_hbm.1, f32[1,64]{1,0:T(1,128)} %bitcast.4, f32[20,128]{1,0:T(8,128)} %bitcast.3, f32[2,64,2560]{2,1,0:T(8,128)} %res_hbm.1), custom_call_target="tpu_custom_call" | custom-call | tf_op jit(solution)/shard_map/pallas_call | solution.py:521
  23.9 0.7 %shard_map.96 = (f32[16,2560]{1,0:T(8,128)}, f32[20,128]{1,0:T(8,128)}) custom-call(f32[16,2560]{1,0:T(8,128)S(1)} %get-tuple-element.6.stitched_ref, f32[20,128]{1,0:T(8,128)S(1)} %get-tuple-element.7.power_ref), custom_call_target="tpu_custom_call" | custom-call | tf_op jit(solution)/shard_map/pallas_call | solution.py:567

commit v8 on v7

--- a/solution.py
+++ b/solution.py
@@ -56,13 +56,19 @@
     return [(a, b - a) for a, b in zip(edges, edges[1:]) if b > a]
 
 
-def kernel(
+def kernel(strips, lanes, *refs):
+    pl.run_scoped(
+        functools.partial(exchange, strips, lanes, *refs), pltpu.SemaphoreType.DMA((7 + refs[7].shape[0],))
+    )
+
+
+def exchange(
     strips, lanes,
     slots_hbm, row_hbm, col_hbm, first_hbm, end_hbm, rows_hbm, cols_hbm, res_hbm,
     out_ref, power_ref,
     slots_ref, row_ref, col_ref, first_ref, end_ref, rows_ref, cols_ref, scale, turned, blocks, inv, xrecv, zsend, zrecv,
     fsend, frecv, fkeep, fxsend, fxrecv, psend, precv,
-    line, sent, xr_sem, zr_sem, fr_sem, gr_sem, pr_sem,
+    line, xr_sem, zr_sem, fr_sem, gr_sem, pr_sem, sent,
 ):
     local, fh, fw = res_hbm.shape
     facets = slots_ref.shape[0]
@@ -72,6 +78,9 @@
     early = fsend.shape[2]
     chunks = column_chunks(tiles, early)
     parts = [(0, early)] + chunks
+    last = len(parts) - 1
+    batch_of = [1 if i == 0 else 2 if i == last else 0 for i in range(len(parts))]
+    batches = [(0, early, chunks[-1][0] - early), (2, *chunks[-1]), (1, *parts[0])][last < 2 :]
     strip = lax.axis_index("strip")
     group = lax.axis_index("col")
     z, x = lax.div(strip, lanes), lax.rem(strip, lanes)
@@ -226,7 +235,7 @@
             src_ref=psend.at[pl.ds(*parts[i])],
             dst_ref=precv.at[k - 1, pl.ds(*parts[i])],
             send_sem=sent.at[4],
-            recv_sem=pr_sem.at[i],
+            recv_sem=pr_sem.at[batch_of[i]],
             device_id={"strip": lax.rem(strip + k, strips)},
             device_id_type=MESH,
         )
@@ -428,7 +437,7 @@
         for j in range(count):
             out_ref[:, pl.ds((first + j) * TILE, TILE)] = stitched[j]
         psend[pl.ds(first, count)] = jnp.sum(stitched * stitched, axis=1, keepdims=True)
-        for k in range(1, strips):
+        for k in sorted(range(1, strips), key=lambda k: -min(k // lanes, levels - k // lanes)):
             p_copy(k, i).start()
 
     for t in range(levels - 1):
@@ -476,8 +485,7 @@
     if strips > 1:
         drain(4, precv)
 
-    for i in list(range(1, len(parts))) + [0]:
-        first, count = parts[i]
+    for i, first, count in batches:
         if strips > 1:
             came = precv.at[:, pl.ds(first, count)]
             pltpu.make_async_remote_copy(
@@ -545,12 +553,11 @@
             pltpu.VMEM((tiles, 1, TILE), jnp.float32),
             pltpu.VMEM((strips - 1, tiles, 1, TILE), jnp.float32),
             pltpu.SemaphoreType.REGULAR((2,)),
-            dma((7 + local,)),
             dma((others, levels, chunks)),
             dma((slots_in, chunks)),
             dma((slots_in,)),
             dma((others,)),
-            dma((chunks + 1,)),
+            dma((3,)),
         ],
         compiler_params=pltpu.CompilerParams(
             collective_id=0,

time: 24.8 us -> 24.7 us (level)
  no operation moved by 1% of the time
where the time goes in v8:
time: 24.7 us; the launch traced here: 24.4 us
  Pallas kernels  23.8 us (96%)
  between operations  0.64 us (3%)
    pallas_call x1, Pallas kernels, body(): pl.pallas_call(functools.partial(kernel, strips, lanes), out_shape=(jax.S...  23.1 us
    pallas_call x1, Pallas kernels, body(): pl.pallas_call(finish, out_shape=(jax.ShapeDtypeStruct((height, fw), jnp....  0.69 us

profile of v8, /device:TPU:0, one launch (start us, length us, event | category | flops | bytes accessed | tf_op | source)
XLA Modules:
  0.0 24.4 jit_solution(17487523808419806590)
XLA Ops:
  0.6 23.1 %shard_map.95 = (f32[16,2560]{1,0:T(8,128)S(1)}, f32[20,128]{1,0:T(8,128)S(1)}) custom-call(s32[16]{0:T(128)} %refs_0_.1, s32[16]{0:T(128)} %refs_1_.1, s32[16]{0:T(128)} %refs_2_.1, s32[16]{0:T(128)} %refs_3_.1, s32[16]{0:T(128)} %refs_4_.1, f32[1,64]{1,0:T(1,128)} %bitcast.4, f32[20,128]{1,0:T(8,128)} %bitcast.3, f32[2,64,2560]{2,1,0:T(8,128)} %refs_7_.1), custom_call_target="tpu_custom_call" | custom-call | tf_op jit(solution)/shard_map/pallas_call | solution.py:529
  23.7 0.7 %shard_map.96 = (f32[16,2560]{1,0:T(8,128)}, f32[20,128]{1,0:T(8,128)}) custom-call(f32[16,2560]{1,0:T(8,128)S(1)} %get-tuple-element.6.stitched_ref, f32[20,128]{1,0:T(8,128)S(1)} %get-tuple-element.7.power_ref), custom_call_target="tpu_custom_call" | custom-call | tf_op jit(solution)/shard_map/pallas_call | solution.py:574

commit v9 on v8

--- a/solution.py
+++ b/solution.py
@@ -109,13 +109,13 @@
         pltpu.make_async_copy(source, target, sent.at[i])
         for i, (source, target) in enumerate(sources)
     ]
-    for load in loads:
-        load.start()
     for p in range(local):
         for i in range(tiles):
             pltpu.make_async_copy(
                 res_hbm.at[p, :, pl.ds(i * TILE, TILE)], turned.at[p, tiles + 1 + i], sent.at[small + p]
             ).start()
+    for load in loads:
+        load.start()
 
     def enter():
         pl.semaphore_wait(barrier, lanes - 1 + low.astype(jnp.int32) + high.astype(jnp.int32))

time: 24.7 us -> 24.7 us (level)
  no operation moved by 1% of the time
where the time goes in v9:
time: 24.7 us; the launch traced here: 24.4 us
  Pallas kernels  23.8 us (96%)
  between operations  0.64 us (3%)
    pallas_call x1, Pallas kernels, body(): pl.pallas_call(functools.partial(kernel, strips, lanes), out_shape=(jax.S...  23.1 us
    pallas_call x1, Pallas kernels, body(): pl.pallas_call(finish, out_shape=(jax.ShapeDtypeStruct((height, fw), jnp....  0.69 us

profile of v9, /device:TPU:0, one launch (start us, length us, event | category | flops | bytes accessed | tf_op | source)
XLA Modules:
  0.0 24.4 jit_solution(10714885576513848881)
XLA Ops:
  0.6 23.1 %shard_map.95 = (f32[16,2560]{1,0:T(8,128)S(1)}, f32[20,128]{1,0:T(8,128)S(1)}) custom-call(s32[16]{0:T(128)} %refs_0_.1, s32[16]{0:T(128)} %refs_1_.1, s32[16]{0:T(128)} %refs_2_.1, s32[16]{0:T(128)} %refs_3_.1, s32[16]{0:T(128)} %refs_4_.1, f32[1,64]{1,0:T(1,128)} %bitcast.4, f32[20,128]{1,0:T(8,128)} %bitcast.3, f32[2,64,2560]{2,1,0:T(8,128)} %refs_7_.1), custom_call_target="tpu_custom_call" | custom-call | tf_op jit(solution)/shard_map/pallas_call | solution.py:529
  23.7 0.7 %shard_map.96 = (f32[16,2560]{1,0:T(8,128)}, f32[20,128]{1,0:T(8,128)}) custom-call(f32[16,2560]{1,0:T(8,128)S(1)} %get-tuple-element.6.stitched_ref, f32[20,128]{1,0:T(8,128)S(1)} %get-tuple-element.7.power_ref), custom_call_target="tpu_custom_call" | custom-call | tf_op jit(solution)/shard_map/pallas_call | solution.py:574
